TPU v7x, 32 devices: a whole 2x2x4 slice. The times are simulated.
32 devices in a mesh: row: 4 (over y, core), col: 8 (over z, x).
Axes of the slice: x: 2, y: 2, z: 4, core: 2. Of those that a mesh axis runs over, the one named last changes fastest.
Arguments:
- features: bfloat16 [32768, 128], P(('row', 'col')), may hold values from -6 to 6
- weight: bfloat16 [128, 128], replicated, may hold values from -0.5 to 0.5
- adj_tiles: bfloat16 [3072, 128, 128], P(('row', 'col')), may hold values from -0.21875 to 0.21875
- tile_rows: int32 [3072], P(('row', 'col')), may hold values from 0 to 63
- tile_cols: int32 [3072], P(('row', 'col')), may hold values from 0 to 31
- tile_count: int32 [32], P(('row', 'col')), may hold values from 24 to 96, as said below
- cotangent: bfloat16 [32768, 128], P(('row', 'col')), may hold values from -6 to 6
Outputs:
- out_features: bfloat16 [32768, 128], P(('row', 'col'))
- weight_grad: float32 [128, 128], replicated
- feature_grad: bfloat16 [32768, 128], P(('row', 'col'))
Inputs may be any that keep to these rules, and one draw needn't show every extreme that they name: Each device has 96 slots, of which the first tile_count are in use; in every draw all devices of at least one row panel use all 96 slots.
All inputs are finite; a program needn't handle non-finite values.
Results may differ from a plain program's by a relative error of at most 0.019.
Values may be sent and summed in bfloat16 or wider, within the bound.
No kernel may reach another device: no remote copies, remote signals or barrier semaphores. Data moves between devices by JAX's collectives and lax.ppermute only.
A program may use at most 128 MiB of HBM per device.

v0:
```python
import jax
import jax.numpy as jnp
from jax import lax
from jax.sharding import PartitionSpec as P


def activate(value):
    return jax.nn.gelu(value, approximate=True)


def activate_grad(pre_act, upstream):
    _, pullback = jax.vjp(activate, pre_act)
    return pullback(upstream)[0]


def tile_pass(summed, tile_values, row_ids, col_ids, live_count, source, backward):
    slot_count = tile_values.shape[0]
    block_size = min(64, slot_count)

    def block_step(block_index, running):
        offset = jnp.minimum(block_index * block_size, slot_count - block_size)
        positions = offset + jnp.arange(block_size, dtype=jnp.int32)
        usable = (positions >= block_index * block_size) & (positions < live_count)
        chosen = lax.dynamic_slice_in_dim(tile_values, offset, block_size, 0)
        chosen = chosen * usable[:, None, None].astype(chosen.dtype)
        row_block = jnp.maximum(lax.dynamic_slice_in_dim(row_ids, offset, block_size, 0), 0)
        col_block = jnp.maximum(lax.dynamic_slice_in_dim(col_ids, offset, block_size, 0), 0)
        if backward:
            product = jnp.einsum(
                "bij,bif->bjf", chosen, source[row_block], preferred_element_type=jnp.float32
            )
            return running.at[col_block].add(product)
        product = jnp.einsum(
            "bij,bjf->bif", chosen, source[col_block], preferred_element_type=jnp.float32
        )
        return running.at[row_block].add(product)

    return lax.fori_loop(0, (live_count + block_size - 1) // block_size, block_step, summed)


def shards(features, weight, adj_tiles, tile_rows, tile_cols, tile_count, cotangent):
    node_dev, feature_width = features.shape
    tile_size = adj_tiles.shape[1]
    panel_tiles = lax.axis_size("col") * node_dev // tile_size
    group_tiles = lax.axis_size("row") * node_dev // tile_size
    live_count = tile_count[0]
    panel_cotangent = lax.all_gather(cotangent, "col", axis=0, tiled=True)
    group_rows = lax.all_gather(features, "row", axis=0, tiled=True).reshape(
        group_tiles, tile_size, feature_width
    )
    summed = jnp.zeros((panel_tiles, tile_size, feature_width), jnp.float32)
    own_values, own_rows, own_cols, own_live = (adj_tiles, tile_rows, tile_cols, live_count)
    summed = tile_pass(summed, own_values, own_rows, own_cols, own_live, group_rows, False)
    panel_partial = summed.reshape(-1, feature_width)
    transposed = (((1,), (1,)), ((), ()))
    panel_total = lax.psum(panel_partial.astype(jnp.bfloat16), "col")
    pre_panel = jnp.dot(panel_total, weight, preferred_element_type=jnp.float32)
    grad_panel = activate_grad(pre_panel, panel_cotangent.astype(jnp.float32)).astype(jnp.bfloat16)
    hidden_grad = lax.dot_general(
        grad_panel, weight, transposed, preferred_element_type=jnp.float32
    ).astype(jnp.bfloat16)
    offset = lax.axis_index("col") * node_dev
    hidden = lax.dynamic_slice_in_dim(panel_total, offset, node_dev, 0)
    pre_act = lax.dynamic_slice_in_dim(pre_panel, offset, node_dev, 0)
    pre_grad = lax.dynamic_slice_in_dim(grad_panel, offset, node_dev, 0)
    out_features = activate(pre_act).astype(jnp.bfloat16)
    weight_term = lax.dot_general(
        hidden, pre_grad, (((0,), (0,)), ((), ())), preferred_element_type=jnp.float32
    )
    weight_grad = lax.psum(weight_term, ("row", "col"))
    grad_tiles = hidden_grad.reshape(panel_tiles, tile_size, feature_width)
    group_grads = jnp.zeros((group_tiles, tile_size, feature_width), jnp.float32)
    group_grads = tile_pass(group_grads, own_values, own_rows, own_cols, own_live, grad_tiles, True)
    feature_grad = lax.psum_scatter(
        group_grads.reshape(-1, feature_width).astype(jnp.bfloat16),
        "row",
        scatter_dimension=0,
        tiled=True,
    )
    return (out_features, weight_grad, feature_grad)


def solution(mesh):
    in_specs = (
        P(("row", "col"), None),
        P(),
        P(("row", "col"), None, None),
        P(("row", "col")),
        P(("row", "col")),
        P(("row", "col")),
        P(("row", "col"), None),
    )
    out_specs = (P(("row", "col"), None), P(), P(("row", "col"), None))
    return jax.shard_map(shards, mesh=mesh, in_specs=in_specs, out_specs=out_specs, check_vma=False)
```

profile of v0, /device:TPU:0, one launch (start us, length us, event | category | flops | bytes accessed | tf_op | source)
XLA Modules:
  0.0 351.7 jit_solution(8370228232801261354)
XLA Ops:
  7.2 0.7 all-gather.3.cloned.1.call-update
  8.0 0.7 all-gather.5.cloned.1.call-update
  9.4 19.6 %all-gather.3.cloned.1.call-done = bf16[4096,128]{1,0:T(8,128)(2,1)} async-done(((bf16[1024,128]{1,0:T(8,128)(2,1)}), bf16[4096,128]{1,0:T(8,128)(2,1)}) %all-gather.3.cloned.1.call-update) | async-done | bytes 1048592 | tf_op jit(solution)/shard_map/all_gather | solution.py:48
  29.0 2.5 broadcast_in_dim.20
  31.5 19.7 %while.20 = (s32[]{:T(128)}, f32[64,128,128]{2,1,0:T(8,128)}, s32[]{:T(128)}, s32[96]{0:T(128)S(1)}, bf16[96,128,128]{2,1,0:T(8,128)(2,1)}, /*index=5*/s32[]{:T(...) while((s32[]{:T(128)}, f32[64,128,128]{2,1,0:T(8,128)}, ...), condition=%wide.region_2.3_spmd, body=%wide.region_0.2_spmd.sunk | while | flops 270534080 | bytes 25172180 | solution.py:38
  31.5 0.1 dynamic-slice_maximum_fusion.6
  31.6 1.0 gather_fusion
  32.6 0.7 and_convert_fusion.4
  33.3 4.3 %fusion.44 = f32[64,128,128]{2,1,0:T(8,128)} fusion(bf16[64,128,128]{2,1,0:T(8,128)(2,1)S(1)} %gather_fusion, bf16[96,128,128]{2,1,0:T(8,128)(2,1)} %get-tuple-element.275, s32[]{:T(128)S(6)} %select_n.29, bf16[64]{0:T(256)(128)(2,1)S(1)} %and_convert_fusion.4), kind=kOutput, calls=%fused_computation.4.clone.1 | convolution fusion | flops 269484032 | bytes 8388740 | tf_op jit(solution)/shard_map/while/body/bij,bjf->bif/dot_general | solution.py:33
  37.6 13.7 %scatter_fusion = f32[64,128,128]{2,1,0:T(8,128)} fusion(f32[64,128,128]{2,1,0:T(8,128)} %get-tuple-element.259, s32[64]{0:T(128)S(1)} %get-tuple-element.233, f32[64,128,128]{2,1,0:T(8,128)} %fusion.44), kind=kCustom, calls=%fused_computation.2.clone.1 | custom fusion | flops 1048576 | bytes 12583168 | tf_op jit(solution)/shard_map/while/body/scatter-add | solution.py:36
  51.2 3.9 %convert_element_type.40 = bf16[64,128,128]{2,1,0:T(8,128)(2,1)} convert(f32[64,128,128]{2,1,0:T(8,128)} %get-tuple-element.89) | non-fusion elementwise | flops 1048576 | bytes 6291456 | tf_op jit(solution)/shard_map/convert_element_type | solution.py:56
  55.2 0.0 all-reduce.5.cloned.1.call-start
  55.2 25.0 %all-gather.5.cloned.1.call-done = bf16[8192,128]{1,0:T(8,128)(2,1)} async-done(((bf16[1024,128]{1,0:T(8,128)(2,1)}), bf16[8192,128]{1,0:T(8,128)(2,1)}) %all-gather.5.cloned.1.call-update) | async-done | bytes 2097168 | tf_op jit(solution)/shard_map/all_gather | solution.py:47
  80.3 104.5 %all-reduce.3.cloned.1.call-done = bf16[8192,128]{1,0:T(8,128)(2,1)} async-done(((bf16[8192,128]{1,0:T(8,128)(2,1)}), bf16[8192,128]{1,0:T(8,128)(2,1)}) %all-reduce.3.cloned.1.call-update) | async-done | bytes 2097168 | tf_op jit(solution)/shard_map/psum | solution.py:56
  184.8 7.2 %fusion.10 = (bf16[8192,128]{1,0:T(8,128)(2,1)S(1)}, f32[8192,128]{1,0:T(8,128)}) fusion(bf16[8192,128]{1,0:T(8,128)(2,1)} %all-gather.5.cloned.1.call-done, bf16[8192,128]{1,0:T(8,128)(2,1)} %all-reduce.3.cloned.1.call-done, bf16[128,128]{1,0:T(8,128)(2,1)S(1)} %copy-done), kind=kOutput, calls=%fused_computation.28 | convolution fusion | flops 290455552 | bytes 10518528 | tf_op jit(solution)/shard_map/dot_general | solution.py:57
  192.0 2.1 convolution_convert_fusion
  194.1 1.9 fusion.26
  195.9 0.0 reduce-scatter.2.cloned.1.call-start
  196.0 0.2 broadcast_in_dim.21
  196.2 25.5 %while.21 = (s32[]{:T(128)}, f32[32,128,128]{2,1,0:T(8,128)S(1)}, s32[]{:T(128)}, s32[96]{0:T(128)S(1)}, bf16[96,128,128]{2,1,0:T(8,128)(2,1)}, /*index=5*/s32[]...) while((s32[]{:T(128)}, f32[32,128,128]{2,1,0:T(8,128)S(1)}, ...), condition=%wide.region_7.8_spmd, body=%wide.region_5.7_spmd.sunk | while | flops 270534080 | bytes 33560784 | solution.py:38
  196.3 0.1 dynamic-slice_maximum_fusion.7
  196.3 3.7 %gather_fusion.1 = bf16[64,128,128]{2,1,0:T(8,128)(2,1)} fusion(bf16[64,128,128]{2,1,0:T(8,128)(2,1)} %get-tuple-element.317, s32[1024]{0:T(1024)S(1)} %pad_clamp_fusion.5), kind=kCustom, calls=%fused_computation.1.clone.1 | custom fusion | bytes 4194560 | tf_op jit(solution)/shard_map/while/body/gather | solution.py:30
  200.1 3.2 constant_dynamic-slice_fusion.2
  203.3 4.1 %copy.13 = bf16[64,128,128]{1,2,0:T(8,128)(2,1)} copy(bf16[64,128,128]{2,1,0:T(8,128)(2,1)} %constant_dynamic-slice_fusion.2) | data formatting | bytes 4194304 | tf_op jit(solution)/shard_map/while/body/dynamic_slice | solution.py:24
  207.3 0.6 and_convert_fusion.5
  208.0 5.0 %fusion.47 = f32[64,128,128]{2,1,0:T(8,128)} fusion(bf16[64,128,128]{2,1,0:T(8,128)(2,1)} %gather_fusion.1, bf16[64,128,128]{1,2,0:T(8,128)(2,1)} %copy.13, bf16[64]{0:T(256)(128)(2,1)S(1)} %and_convert_fusion.5), kind=kOutput, calls=%fused_computation.13.clone.1 | convolution fusion | flops 269484032 | bytes 8388736 | tf_op jit(solution)/shard_map/while/body/bij,bif->bjf/dot_general | solution.py:29
  212.9 8.8 %scatter_fusion.1 = f32[32,128,128]{2,1,0:T(8,128)S(1)} fusion(f32[32,128,128]{2,1,0:T(8,128)S(1)} %get-tuple-element.298, s32[64]{0:T(128)S(1)} %get-tuple-element.243, f32[64,128,128]{2,1,0:T(8,128)} %fusion.47), kind=kCustom, calls=%fused_computation.3.clone.1 | custom fusion | flops 1048576 | bytes 12583168 | tf_op jit(solution)/shard_map/while/body/scatter-add | solution.py:32
  221.8 1.1 convert_element_type.46
  222.9 1.9 fusion.25
  224.8 89.9 %all-reduce.5.cloned.1.call-done = f32[128,128]{1,0:T(8,128)} async-done(((f32[128,128]{1,0:T(8,128)}), f32[128,128]{1,0:T(8,128)}) %all-reduce.5.cloned.1.call-update) | async-done | bytes 65552 | tf_op jit(solution)/shard_map/psum | solution.py:70
  314.7 29.0 %reduce-scatter.2.cloned.1.call-done = bf16[1024,128]{1,0:T(8,128)(2,1)} async-done(((bf16[4096,128]{1,0:T(8,128)(2,1)}), bf16[1024,128]{1,0:T(8,128)(2,1)}) %reduce-scatter.2.cloned.1.call-update) | async-done | bytes 262160 | tf_op jit(solution)/shard_map/reduce_scatter | solution.py:74
  343.7 1.5 copy.31
  (16 shorter events, 0.2 us)
Async XLA Ops:
  7.2 177.6 %copy-start = (bf16[128,128]{1,0:T(8,128)(2,1)S(1)}, bf16[128,128]{1,0:T(8,128)(2,1)}, u32[]{:S(2)}) copy-start(bf16[128,128]{1,0:T(8,128)(2,1)} %param.12) | copy-start | bytes 98308
  7.2 24.3 %copy-start.2 = (s32[96]{0:T(128)S(1)}, s32[96]{0:T(128)}, u32[]{:S(2)}) copy-start(s32[96]{0:T(128)} %param.14) | copy-start | bytes 1156
  7.2 24.3 %copy-start.3 = (s32[96]{0:T(128)S(1)}, s32[96]{0:T(128)}, u32[]{:S(2)}) copy-start(s32[96]{0:T(128)} %param.15) | copy-start | bytes 1156
  7.2 21.8 %all-gather.3.cloned.1.call-start = ((), (), s32[]{:S(2)}) async-start(), calls=%async_computation.1 | async-start | bytes 1310720 | tf_op jit(solution)/shard_map/all_gather | solution.py:48
  7.9 72.3 %all-gather.5.cloned.1.call-start = ((), (), s32[]{:S(2)}) async-start(), calls=%async_computation.3 | async-start | bytes 2359296 | tf_op jit(solution)/shard_map/all_gather | solution.py:47
  8.7 176.1 %all-reduce.3.cloned.1.call-start = ((), (), s32[]{:S(2)}) async-start(), calls=%async_computation.2 | async-start | bytes 4194304 | tf_op jit(solution)/shard_map/psum | solution.py:56
  29.0 2.5 copy-start.1
  55.2 259.5 %all-reduce.5.cloned.1.call-start = ((), (), s32[]{:S(2)}) async-start(), calls=%async_computation.4 | async-start | bytes 131072 | tf_op jit(solution)/shard_map/psum | solution.py:70
  195.9 147.8 %reduce-scatter.2.cloned.1.call-start = ((), (), s32[]{:S(2)}) async-start(), calls=%async_computation.5 | async-start | bytes 1310720 | tf_op jit(solution)/shard_map/reduce_scatter | solution.py:74
Sparse Core Ops, SparseCore 0:
  9.6 19.4 all-gather.2
  31.1 49.0 all-gather.4
  83.9 100.8 all-reduce.2
  196.1 118.5 all-reduce.4
  317.6 26.0 reduce-scatter.1
where the time goes:
time: 353 us; the launch traced here: 352 us
  waiting for transfers between devices  269 us (76%)
  other arithmetic  30.9 us (9%)
  matrix products  20.4 us (6%)
  local copies, waits for them, and re-layouts  16.1 us (5%)
  between operations  14.5 us (4%)
    psum x1, waiting for transfers between devices, shards(): panel_total = lax.psum(panel_partial.astype(jnp.bfloat16), 'col')  104 us
    psum x1, waiting for transfers between devices, shards(): weight_grad = lax.psum(weight_term, ('row', 'col'))  89.9 us
    reduce_scatter x1, waiting for transfers between devices, shards(): lax.psum_scatter(group_grads.reshape(-1, feature_width).astype(jnp.bfloat...  29 us
    all_gather x1, waiting for transfers between devices, shards(): panel_cotangent = lax.all_gather(cotangent, 'col', axis=0, tiled=True)  25 us
    all_gather x1, waiting for transfers between devices, shards(): lax.all_gather(features, 'row', axis=0, tiled=True)  19.6 us
    scatter-add x1, other arithmetic, block_step(): return running.at[row_block].add(product)  13.7 us
    scatter-add x1, other arithmetic, block_step(): return running.at[col_block].add(product)  8.81 us
    dynamic_slice x2, local copies, waits for them, and re-layouts, block_step(): chosen = lax.dynamic_slice_in_dim(tile_values, offset, block_size, 0)  7.23 us
  transfers between devices with their start and end apart: 5, of which 5 were waited for; matrix products, arithmetic and copies ran while one was open for 16% of the time, Pallas kernels for 0%

commit v1 on v0

v1 whole, which is shorter than its diff:
```python
import functools

import jax
import jax.numpy as jnp
from jax import lax
from jax.experimental import pallas as pl
from jax.experimental.pallas import tpu as pltpu
from jax.sharding import PartitionSpec as P

UNROLL = 4
F32 = jnp.float32
BF16 = jnp.bfloat16
GELU_SCALE = 0.7978845608028654
GELU_CUBIC = 0.044715


def permute_xor(value, axis, mask):
    size = lax.axis_size(axis)
    return lax.ppermute(value, axis, [(i, i ^ mask) for i in range(size)])


def gather_pieces(value, axis):
    size = lax.axis_size(axis)
    pieces = [None] * size
    pieces[0] = value
    for major in list(range(4, size, 2)) + [2]:
        if major < size:
            pieces[major] = permute_xor(value, axis, major)
    for major in [0] + list(range(4, size, 2)) + [2]:
        if major < size:
            pieces[major + 1] = permute_xor(pieces[major], axis, 1)
    return pieces


def scatter_pieces(parts, axis):
    size = len(parts)
    terms = [parts[0]]
    for major in list(range(4, size, 2)) + [2]:
        if major < size:
            received = permute_xor(parts[major + 1], axis, 1)
            joined = (parts[major].astype(F32) + received.astype(F32)).astype(BF16)
            terms.append(permute_xor(joined, axis, major))
    terms.append(permute_xor(parts[1], axis, 1))
    return terms


def all_sum(value, axes):
    for axis in axes:
        mask = 1
        while mask < lax.axis_size(axis):
            value = value + permute_xor(value, axis, mask)
            mask *= 2
    return value


def tile_kernel(n_src, n_out, tile_size, slots, to_rows, *refs):
    rows_ref, cols_ref, count_ref, ids_ref, adj_hbm = refs[:5]
    sources = refs[5 : 5 + n_src]
    outs = refs[5 + n_src : 5 + n_src + n_out]
    adj, source, acc, sems = refs[5 + n_src + n_out :]
    src_id = ids_ref[0]
    out_id = ids_ref[1]
    adj_copy = pltpu.make_async_copy(adj_hbm, adj, sems.at[n_src])
    adj_copy.start()
    copies = []
    for r in range(n_src):
        copy = pltpu.make_async_copy(sources[r], source.at[src_id ^ r], sems.at[r])
        copy.start()
        copies.append(copy)
    out_tiles = n_out * outs[0].shape[0]
    src_tiles = source.shape[1]
    acc[...] = jnp.zeros(acc.shape, F32)
    for copy in copies:
        copy.wait()
    adj_copy.wait()
    count = count_ref[0]

    def step(block, carry):
        products = []
        for u in range(UNROLL):
            slot = block * UNROLL + u
            at = jnp.minimum(slot, slots - 1)
            if to_rows:
                target, origin = rows_ref[at], cols_ref[at]
            else:
                target, origin = cols_ref[at], rows_ref[at]
            target = jnp.where(slot < count, target, out_tiles)
            piece = source[origin // src_tiles, origin % src_tiles]
            if to_rows:
                product = jnp.dot(adj[at], piece, preferred_element_type=F32)
            else:
                product = jnp.dot(piece, adj[at], preferred_element_type=F32)
            products.append((target, product))
        for target, product in products:
            acc[target] = acc[target] + product
        return carry

    lax.fori_loop(0, (count + UNROLL - 1) // UNROLL, step, 0)
    for r in range(n_out):
        tiles = outs[r].shape[0]
        outs[r][...] = acc[pl.ds((out_id ^ r) * tiles, tiles)].astype(BF16)


def tile_pass(rows, cols, count, ids, adj_tiles, pieces, n_out, out_tiles, to_rows):
    slots, tile_size, _ = adj_tiles.shape
    n_src = len(pieces)
    block = pieces[0].shape
    width = block[-1]
    smem = pl.BlockSpec(memory_space=pltpu.SMEM)
    hbm = pl.BlockSpec(memory_space=pl.ANY)
    vmem = pl.BlockSpec(memory_space=pltpu.VMEM)
    return pl.pallas_call(
        functools.partial(tile_kernel, n_src, n_out, tile_size, slots, to_rows),
        in_specs=[smem] * 4 + [hbm] * (1 + n_src),
        out_specs=[vmem] * n_out,
        out_shape=[jax.ShapeDtypeStruct((out_tiles, tile_size, width), BF16)] * n_out,
        scratch_shapes=[
            pltpu.VMEM(adj_tiles.shape, BF16),
            pltpu.VMEM((n_src,) + block, BF16),
            pltpu.VMEM((n_out * out_tiles + 1, tile_size, width), F32),
            pltpu.SemaphoreType.DMA((n_src + 1,)),
        ],
    )(rows, cols, count, ids, adj_tiles, *pieces)


def middle_kernel(n_terms, *refs):
    terms = refs[:n_terms]
    weight_ref, cot_ref, out_ref, grad_ref, wterm_ref = refs[n_terms:]
    weight = weight_ref[...]
    wterm = None
    for t in range(cot_ref.shape[0]):
        total = terms[0][t].astype(F32)
        for term in terms[1:]:
            total = total + term[t].astype(F32)
        hidden = total.astype(BF16)
        pre = jnp.dot(hidden, weight, preferred_element_type=F32)
        square = pre * pre
        tanh = jnp.tanh(GELU_SCALE * (pre + GELU_CUBIC * square * pre))
        half = 0.5 * (1.0 + tanh)
        out_ref[t] = (pre * half).astype(BF16)
        slope = half + 0.5 * pre * (1.0 - tanh * tanh) * (
            GELU_SCALE * (1.0 + 3.0 * GELU_CUBIC * square)
        )
        grad = (cot_ref[t].astype(F32) * slope).astype(BF16)
        grad_ref[t] = lax.dot_general(
            weight, grad, (((1,), (1,)), ((), ())), preferred_element_type=F32
        ).astype(BF16)
        part = lax.dot_general(
            hidden, grad, (((0,), (0,)), ((), ())), preferred_element_type=F32
        )
        wterm = part if wterm is None else wterm + part
    wterm_ref[...] = wterm


def middle(terms, weight, cotangent):
    return pl.pallas_call(
        functools.partial(middle_kernel, len(terms)),
        out_shape=[
            jax.ShapeDtypeStruct(cotangent.shape, BF16),
            jax.ShapeDtypeStruct(cotangent.shape, BF16),
            jax.ShapeDtypeStruct(weight.shape, F32),
        ],
    )(*terms, weight, cotangent)


def final_kernel(n_terms, *refs):
    terms, out_ref = refs[:n_terms], refs[n_terms]
    for t in range(out_ref.shape[0]):
        total = terms[0][t].astype(F32)
        for term in terms[1:]:
            total = total + term[t].astype(F32)
        out_ref[t] = total.T.astype(BF16)


def final(terms):
    return pl.pallas_call(
        functools.partial(final_kernel, len(terms)),
        out_shape=jax.ShapeDtypeStruct(terms[0].shape, BF16),
    )(*terms)


def shards(features, weight, adj_tiles, tile_rows, tile_cols, tile_count, cotangent):
    node_dev, width = features.shape
    tile_size = adj_tiles.shape[1]
    dev_tiles = node_dev // tile_size
    as_tiles = (dev_tiles, tile_size, width)
    row_id = lax.axis_index("row").astype(jnp.int32)
    col_id = lax.axis_index("col").astype(jnp.int32)
    table = (tile_rows, tile_cols, tile_count)
    group = gather_pieces(features.reshape(as_tiles), "row")
    parts = tile_pass(
        *table, jnp.stack([row_id, col_id]), adj_tiles, group, lax.axis_size("col"), dev_tiles, True
    )
    terms = scatter_pieces(parts, "col")
    out_features, grad, wterm = middle(terms, weight, cotangent.reshape(as_tiles))
    panel = gather_pieces(grad, "col")
    weight_grad = all_sum(wterm, ("row", "col"))
    parts = tile_pass(
        *table, jnp.stack([col_id, row_id]), adj_tiles, panel, lax.axis_size("row"), dev_tiles, False
    )
    feature_grad = final(scatter_pieces(parts, "row"))
    return (
        out_features.reshape(node_dev, width),
        weight_grad,
        feature_grad.reshape(node_dev, width),
    )


def solution(mesh):
    in_specs = (
        P(("row", "col"), None),
        P(),
        P(("row", "col"), None, None),
        P(("row", "col")),
        P(("row", "col")),
        P(("row", "col")),
        P(("row", "col"), None),
    )
    out_specs = (P(("row", "col"), None), P(), P(("row", "col"), None))
    return jax.shard_map(shards, mesh=mesh, in_specs=in_specs, out_specs=out_specs, check_vma=False)
```

time: 353 us -> 131 us (0.37)
  waiting for transfers between devices: 269 us -> 69.3 us
  starting transfers between devices: 0.2 us -> 34.3 us
  other arithmetic: 30.9 us -> 6 us
  matrix products: 20.4 us -> 0 us
  Pallas kernels: 0 us -> 16.5 us
  between operations: 14.5 us -> 1.44 us
  local copies, waits for them, and re-layouts: 16.1 us -> 3.36 us
    psum x2 -> x0, waiting for transfers between devices: 194 us -> none  [the longest x1 104 us: shards(): panel_total = lax.psum(panel_partial.astype(jnp.bfloat16), 'col')]
    ppermute x0 -> x25, waiting for transfers between devices: none -> 69.3 us  [permute_xor(): return lax.ppermute(value, axis, [(i, i ^ mask) for i in range(size)])]
    all_gather x2 -> x0, waiting for transfers between devices: 44.7 us -> none  [the longest x1 25 us: shards(): panel_cotangent = lax.all_gather(cotangent, 'col', axis=0, tiled=True)]
    ppermute x0 -> x25, starting transfers between devices: none -> 34.3 us  [permute_xor(): return lax.ppermute(value, axis, [(i, i ^ mask) for i in range(size)])]
    reduce_scatter x1 -> x0, waiting for transfers between devices: 29 us -> none  [shards(): lax.psum_scatter(group_grads.reshape(-1, feature_width).astype(jnp.bfloat...]
    scatter-add x2 -> x0, other arithmetic: 22.5 us -> none  [the longest x1 13.7 us: block_step(): return running.at[row_block].add(product)]
    dot_general x5 -> x0, matrix products: 20.4 us -> none  [the longest x1 7.22 us: shards(): pre_panel = jnp.dot(panel_total, weight, preferred_element_type=jnp.float32)]
    pallas_call x0 -> x4, Pallas kernels: none -> 16.5 us  [the longest x2 11.3 us: tile_pass(): pl.pallas_call(functools.partial(tile_kernel, n_src, n_out, tile_size, sl...]
  transfers between devices with their start and end apart: 5 -> 25, of which waited for: 5 -> 16; matrix products, arithmetic and copies ran while one was open for 16% -> 5% of each run, Pallas kernels for 0% -> 0%
where the time goes in v1:
time: 131 us
  waiting for transfers between devices  69.3 us (53%)
  starting transfers between devices  34.3 us (26%)
  Pallas kernels  16.5 us (13%)
  other arithmetic  6 us (5%)
  local copies, waits for them, and re-layouts  3.36 us (3%)
  between operations  1.44 us (1%)
    ppermute x25, waiting for transfers between devices, permute_xor(): return lax.ppermute(value, axis, [(i, i ^ mask) for i in range(size)])  69.3 us
    ppermute x25, starting transfers between devices, permute_xor(): return lax.ppermute(value, axis, [(i, i ^ mask) for i in range(size)])  34.3 us
    pallas_call x2, Pallas kernels, tile_pass(): pl.pallas_call(functools.partial(tile_kernel, n_src, n_out, tile_size, sl...  11.3 us
    convert_element_type x4, other arithmetic, scatter_pieces(): joined = (parts[major].astype(F32) + received.astype(F32)).astype(BF16)  4.1 us
    unnamed x34, local copies, waits for them, and re-layouts  3.36 us
    pallas_call x1, Pallas kernels, middle(): pl.pallas_call(functools.partial(middle_kernel, len(terms)), out_shape=[j...  3.2 us
  transfers between devices with their start and end apart: 25, of which 16 were waited for; matrix products, arithmetic and copies ran while one was open for 5% of the time, Pallas kernels for 0%

profile of v1, /device:TPU:0, one launch (start us, length us, event | category | flops | bytes accessed | tf_op | source)
XLA Modules:
  0.0 130.9 jit_solution(1041631565293770320)
XLA Ops:
  0.6 3.1 %collective-permute-start.1 = (bf16[8,128,128]{2,1,0:T(8,128)(2,1)}, bf16[8,128,128]{2,1,0:T(8,128)(2,1)S(1)}, u32[]{:S(2)}, u32[]{:S(2)}) collective-permute-start(bf16[8,128,128]{2,1,0:T(8,128)(2,1)} %bitcast.8), channel_id=1, source_target_pairs={{0,16},{8,24},{16,0},{24,8},{1,17},{9,25},{17,1},{25,9},{2,18},{10... | collective-permute-start | bytes 786440 | tf_op jit(solution)/shard_map/ppermute | solution.py:19
  3.7 6.5 %collective-permute-done.1.refs_7_ = bf16[8,128,128]{2,1,0:T(8,128)(2,1)S(1)} collective-permute-done((bf16[8,128,128]{2,1,0:T(8,128)(2,1)}, bf16[8,128,128]{2,1,0:T(8,128)(2,1)S(1)}, u32[]{:S(2)}, u32[]{:S(2)}) %collective-permute-start.1) | collective-permute-done | bytes 262176 | tf_op jit(solution)/shard_map/ppermute | solution.py:19
  12.9 5.7 %shard_map.94 = (bf16[8,128,128]{2,1,0:T(8,128)(2,1)}, bf16[8,128,128]{2,1,0:T(8,128)(2,1)}, bf16[8,128,128]{2,1,0:T(8,128)(2,1)}, bf16[8,128,128]{2,1,0:T(8,128...) custom-call(s32[96]{0:T(128)} %refs_0_.3, ...), custom_call_target="tpu_custom_call" | custom-call | tf_op jit(solution)/shard_map/pallas_call | solution.py:112
  18.6 2.0 %collective-permute-start.3 = (bf16[8,128,128]{2,1,0:T(8,128)(2,1)}, bf16[8,128,128]{2,1,0:T(8,128)(2,1)S(1)}, u32[]{:S(2)}, u32[]{:S(2)}) collective-permute-start(bf16[8,128,128]{2,1,0:T(8,128)(2,1)} %get-tuple-element.20), channel_id=1, source_target_pairs={{0,1},{1,0},{2,3},{3,2},{4,5},{5,4},{6,7},{7,6},{8,9},{9,8},{10,11... | collective-permute-start | bytes 786440 | tf_op jit(solution)/shard_map/ppermute | solution.py:19
  20.7 1.9 %collective-permute-start.7 = (bf16[8,128,128]{2,1,0:T(8,128)(2,1)}, bf16[8,128,128]{2,1,0:T(8,128)(2,1)S(1)}, u32[]{:S(2)}, u32[]{:S(2)}) collective-permute-start(bf16[8,128,128]{2,1,0:T(8,128)(2,1)} %get-tuple-element.24), channel_id=1, source_target_pairs={{0,1},{1,0},{2,3},{3,2},{4,5},{5,4},{6,7},{7,6},{8,9},{9,8},{10,11... | collective-permute-start | bytes 786440 | tf_op jit(solution)/shard_map/ppermute | solution.py:19
  22.7 2.5 %collective-permute-done.3 = bf16[8,128,128]{2,1,0:T(8,128)(2,1)S(1)} collective-permute-done((bf16[8,128,128]{2,1,0:T(8,128)(2,1)}, bf16[8,128,128]{2,1,0:T(8,128)(2,1)S(1)}, u32[]{:S(2)}, u32[]{:S(2)}) %collective-permute-start.3) | collective-permute-done | bytes 262176 | tf_op jit(solution)/shard_map/ppermute | solution.py:19
  25.2 1.0 add_convert_fusion.3
  26.3 4.4 %collective-permute-start.4 = (bf16[8,128,128]{2,1,0:T(8,128)(2,1)S(1)}, bf16[8,128,128]{2,1,0:T(8,128)(2,1)S(1)}, u32[]{:S(2)}, u32[]{:S(2)}) collective-permute-start(bf16[8,128,128]{2,1,0:T(8,128)(2,1)S(1)} %add_convert_fusion.3), channel_id=1, source_target_pairs={{0,4},{1,5},{2,6},{3,7},{4,0},{5,1},{6,2},{7,3},{8,12},{9,13},{10,... | collective-permute-start | bytes 786440 | tf_op jit(solution)/shard_map/ppermute | solution.py:19
  30.8 1.0 add_convert_fusion.2
  31.8 5.8 %collective-permute-start.6 = (bf16[8,128,128]{2,1,0:T(8,128)(2,1)S(1)}, bf16[8,128,128]{2,1,0:T(8,128)(2,1)S(1)}, u32[]{:S(2)}, u32[]{:S(2)}) collective-permute-start(bf16[8,128,128]{2,1,0:T(8,128)(2,1)S(1)} %add_convert_fusion.2), channel_id=1, source_target_pairs={{0,6},{1,7},{2,4},{3,5},{4,2},{5,3},{6,0},{7,1},{8,14},{9,15},{10,... | collective-permute-start | bytes 786440 | tf_op jit(solution)/shard_map/ppermute | solution.py:19
  37.7 1.0 add_convert_fusion.1
  38.7 2.2 %collective-permute-start.8 = (bf16[8,128,128]{2,1,0:T(8,128)(2,1)S(1)}, bf16[8,128,128]{2,1,0:T(8,128)(2,1)S(1)}, u32[]{:S(2)}, u32[]{:S(2)}) collective-permute-start(bf16[8,128,128]{2,1,0:T(8,128)(2,1)S(1)} %add_convert_fusion.1), channel_id=1, source_target_pairs={{0,2},{1,3},{2,0},{3,1},{4,6},{5,7},{6,4},{7,5},{8,10},{9,11},{10,... | collective-permute-start | bytes 786440 | tf_op jit(solution)/shard_map/ppermute | solution.py:19
  40.9 1.2 collective-permute-done.9.refs_4_
  42.1 5.6 %collective-permute-done.4.refs_1_ = bf16[8,128,128]{2,1,0:T(8,128)(2,1)S(1)} collective-permute-done((bf16[8,128,128]{2,1,0:T(8,128)(2,1)S(1)}, bf16[8,128,128]{2,1,0:T(8,128)(2,1)S(1)}, u32[]{:S(2)}, u32[]{:S(2)}) %collective-permute-start.4) | collective-permute-done | bytes 262176 | tf_op jit(solution)/shard_map/ppermute | solution.py:19
  47.7 6.9 %collective-permute-done.8.refs_3_ = bf16[8,128,128]{2,1,0:T(8,128)(2,1)S(1)} collective-permute-done((bf16[8,128,128]{2,1,0:T(8,128)(2,1)S(1)}, bf16[8,128,128]{2,1,0:T(8,128)(2,1)S(1)}, u32[]{:S(2)}, u32[]{:S(2)}) %collective-permute-start.8) | collective-permute-done | bytes 262176 | tf_op jit(solution)/shard_map/ppermute | solution.py:19
  55.3 3.2 %shard_map.95 = (bf16[8,128,128]{2,1,0:T(8,128)(2,1)}, bf16[8,128,128]{2,1,0:T(8,128)(2,1)}, f32[128,128]{1,0:T(8,128)}) custom-call(bf16[8,128,128]{2,1,0:T(8,128)(2,1)} %get-tuple-element.18.refs_0_, bf16[8,128,128]{2,1,0:T(8,128)(2,1)} %copy-done.5, bf16[8,128,128]{2,1,0:T(8,128)(2,1)} %copy-done.7, bf16[8,128,128]{2,1,0:T(8,128)(2,1)} %copy-done.10, ...), custom_call_target="tpu_custom_call" | custom-call | tf_op jit(solution)/shard_map/pallas_call | solution.py:156
  58.5 3.8 %collective-permute-start.20 = (bf16[8,128,128]{2,1,0:T(8,128)(2,1)}, bf16[8,128,128]{2,1,0:T(8,128)(2,1)S(1)}, u32[]{:S(2)}, u32[]{:S(2)}) collective-permute-start(bf16[8,128,128]{2,1,0:T(8,128)(2,1)} %get-tuple-element.28.refs_5_), channel_id=1, source_target_pairs={{0,6},{1,7},{2,4},{3,5},{4,2},{5,3},{6,0},{7,1},{8,14},{9,15},{10,... | collective-permute-start | bytes 786440 | tf_op jit(solution)/shard_map/ppermute | solution.py:19
  63.6 6.2 %collective-permute-done.20.refs_11_ = bf16[8,128,128]{2,1,0:T(8,128)(2,1)S(1)} collective-permute-done((bf16[8,128,128]{2,1,0:T(8,128)(2,1)}, bf16[8,128,128]{2,1,0:T(8,128)(2,1)S(1)}, u32[]{:S(2)}, u32[]{:S(2)}) %collective-permute-start.20) | collective-permute-done | bytes 262176 | tf_op jit(solution)/shard_map/ppermute | solution.py:19
  70.5 14.5 %collective-permute-done.18.refs_9_ = bf16[8,128,128]{2,1,0:T(8,128)(2,1)S(1)} collective-permute-done((bf16[8,128,128]{2,1,0:T(8,128)(2,1)}, bf16[8,128,128]{2,1,0:T(8,128)(2,1)S(1)}, u32[]{:S(2)}, u32[]{:S(2)}) %collective-permute-start.18) | collective-permute-done | bytes 262176 | tf_op jit(solution)/shard_map/ppermute | solution.py:19
  85.0 2.0 %collective-permute-start.17 = (bf16[8,128,128]{2,1,0:T(8,128)(2,1)S(1)}, bf16[8,128,128]{2,1,0:T(8,128)(2,1)S(1)}, u32[]{:S(2)}, u32[]{:S(2)}) collective-permute-start(bf16[8,128,128]{2,1,0:T(8,128)(2,1)S(1)} %collective-permute-done.16.refs_7_), channel_id=1, source_target_pairs={{0,1},{1,0},{2,3},{3,2},{4,5},{5,4},{6,7},{7,6},{8,9},{9,8},{10,11... | collective-permute-start | bytes 786440 | tf_op jit(solution)/shard_map/ppermute | solution.py:19
  87.7 6.5 %collective-permute-done.19.refs_10_ = bf16[8,128,128]{2,1,0:T(8,128)(2,1)S(1)} collective-permute-done((bf16[8,128,128]{2,1,0:T(8,128)(2,1)S(1)}, bf16[8,128,128]{2,1,0:T(8,128)(2,1)S(1)}, u32[]{:S(2)}, u32[]{:S(2)}) %collective-permute-start.19) | collective-permute-done | bytes 262176 | tf_op jit(solution)/shard_map/ppermute | solution.py:19
  94.2 4.4 %collective-permute-done.17.refs_8_ = bf16[8,128,128]{2,1,0:T(8,128)(2,1)S(1)} collective-permute-done((bf16[8,128,128]{2,1,0:T(8,128)(2,1)S(1)}, bf16[8,128,128]{2,1,0:T(8,128)(2,1)S(1)}, u32[]{:S(2)}, u32[]{:S(2)}) %collective-permute-start.17) | collective-permute-done | bytes 262176 | tf_op jit(solution)/shard_map/ppermute | solution.py:19
  99.3 5.6 %shard_map.96 = (bf16[8,128,128]{2,1,0:T(8,128)(2,1)}, bf16[8,128,128]{2,1,0:T(8,128)(2,1)}, bf16[8,128,128]{2,1,0:T(8,128)(2,1)}, bf16[8,128,128]{2,1,0:T(8,128)(2,1)}) custom-call(s32[96]{0:T(128)} %refs_0_.3, s32[96]{0:T(128)} %refs_1_.3, s32[1]{0:T(128)S(6)} %copy.10.refs_2_, s32[2]{0:T(128)} %pad_add_fusion.1.refs_3_, bf16[96,128,128]{2,1,0:T(8,128)(2,1)} %refs_4_.3, ...), custom_call_target="tpu_custom_call" | custom-call | tf_op jit(solution)/shard_map/pallas_call | solution.py:112
  104.9 2.0 %collective-permute-start.22 = (bf16[8,128,128]{2,1,0:T(8,128)(2,1)}, bf16[8,128,128]{2,1,0:T(8,128)(2,1)S(1)}, u32[]{:S(2)}, u32[]{:S(2)}) collective-permute-start(bf16[8,128,128]{2,1,0:T(8,128)(2,1)} %get-tuple-element.31), channel_id=1, source_target_pairs={{0,8},{8,0},{16,24},{24,16},{1,9},{9,1},{17,25},{25,17},{2,10},{10... | collective-permute-start | bytes 786440 | tf_op jit(solution)/shard_map/ppermute | solution.py:19
  107.0 1.4 %collective-permute-done.10 = f32[128,128]{1,0:T(8,128)S(1)} collective-permute-done((f32[128,128]{1,0:T(8,128)S(1)}, f32[128,128]{1,0:T(8,128)S(1)}, u32[]{:S(2)}, u32[]{:S(2)}) %collective-permute-start.10) | collective-permute-done | bytes 65568 | tf_op jit(solution)/shard_map/ppermute | solution.py:19
  109.0 1.0 add_convert_fusion
  110.0 1.7 %collective-permute-start.23 = (bf16[8,128,128]{2,1,0:T(8,128)(2,1)S(1)}, bf16[8,128,128]{2,1,0:T(8,128)(2,1)S(1)}, u32[]{:S(2)}, u32[]{:S(2)}) collective-permute-start(bf16[8,128,128]{2,1,0:T(8,128)(2,1)S(1)} %add_convert_fusion), channel_id=1, source_target_pairs={{0,16},{8,24},{16,0},{24,8},{1,17},{9,25},{17,1},{25,9},{2,18},{10... | collective-permute-start | bytes 786440 | tf_op jit(solution)/shard_map/ppermute | solution.py:19
  111.7 1.2 collective-permute-done.11
  113.5 3.7 %collective-permute-done.12 = f32[128,128]{1,0:T(8,128)S(1)} collective-permute-done((f32[128,128]{1,0:T(8,128)S(1)}, f32[128,128]{1,0:T(8,128)S(1)}, u32[]{:S(2)}, u32[]{:S(2)}) %collective-permute-start.12) | collective-permute-done | bytes 65568 | tf_op jit(solution)/shard_map/ppermute | solution.py:19
  118.2 3.4 %collective-permute-done.13 = f32[128,128]{1,0:T(8,128)S(1)} collective-permute-done((f32[128,128]{1,0:T(8,128)S(1)}, f32[128,128]{1,0:T(8,128)S(1)}, u32[]{:S(2)}, u32[]{:S(2)}) %collective-permute-start.13) | collective-permute-done | bytes 65568 | tf_op jit(solution)/shard_map/ppermute | solution.py:19
  122.5 5.0 %collective-permute-done.14 = f32[128,128]{1,0:T(8,128)S(1)} collective-permute-done((f32[128,128]{1,0:T(8,128)S(1)}, f32[128,128]{1,0:T(8,128)S(1)}, u32[]{:S(2)}, u32[]{:S(2)}) %collective-permute-start.14) | collective-permute-done | bytes 65568 | tf_op jit(solution)/shard_map/ppermute | solution.py:19
  129.0 2.0 %shard_map.97 = bf16[8,128,128]{2,1,0:T(8,128)(2,1)} custom-call(bf16[8,128,128]{2,1,0:T(8,128)(2,1)} %get-tuple-element.29.refs_0_, bf16[8,128,128]{2,1,0:T(8,128)(2,1)} %copy-done.12, bf16[8,128,128]{2,1,0:T(8,128)(2,1)} %copy-done.11), custom_call_target="tpu_custom_call" | custom-call | tf_op jit(solution)/shard_map/pallas_call | solution.py:176
  (67 shorter events, 11.1 us)
Async XLA Ops:
  0.6 9.6 %collective-permute-start.1 = (bf16[8,128,128]{2,1,0:T(8,128)(2,1)}, bf16[8,128,128]{2,1,0:T(8,128)(2,1)S(1)}, u32[]{:S(2)}, u32[]{:S(2)}) collective-permute-start(bf16[8,128,128]{2,1,0:T(8,128)(2,1)} %bitcast.8), channel_id=1, source_target_pairs={{0,16},{8,24},{16,0},{24,8},{1,17},{9,25},{17,1},{25,9},{2,18},{10... | collective-permute-start | bytes 786440 | tf_op jit(solution)/shard_map/ppermute | solution.py:19
  3.7 7.8 %collective-permute-start = (bf16[8,128,128]{2,1,0:T(8,128)(2,1)}, bf16[8,128,128]{2,1,0:T(8,128)(2,1)S(1)}, u32[]{:S(2)}, u32[]{:S(2)}) collective-permute-start(bf16[8,128,128]{2,1,0:T(8,128)(2,1)} %bitcast.9), channel_id=1, source_target_pairs={{0,8},{8,0},{16,24},{24,16},{1,9},{9,1},{17,25},{25,17},{2,10},{10... | collective-permute-start | bytes 786440 | tf_op jit(solution)/shard_map/ppermute | solution.py:19
  10.2 1.5 %collective-permute-start.2 = (bf16[8,128,128]{2,1,0:T(8,128)(2,1)S(1)}, bf16[8,128,128]{2,1,0:T(8,128)(2,1)S(1)}, u32[]{:S(2)}, u32[]{:S(2)}) collective-permute-start(bf16[8,128,128]{2,1,0:T(8,128)(2,1)S(1)} %collective-permute-done.1.refs_7_), channel_id=1, source_target_pairs={{0,8},{8,0},{16,24},{24,16},{1,9},{9,1},{17,25},{25,17},{2,10},{10... | collective-permute-start | bytes 786440 | tf_op jit(solution)/shard_map/ppermute | solution.py:19
  18.6 6.6 %collective-permute-start.3 = (bf16[8,128,128]{2,1,0:T(8,128)(2,1)}, bf16[8,128,128]{2,1,0:T(8,128)(2,1)S(1)}, u32[]{:S(2)}, u32[]{:S(2)}) collective-permute-start(bf16[8,128,128]{2,1,0:T(8,128)(2,1)} %get-tuple-element.20), channel_id=1, source_target_pairs={{0,1},{1,0},{2,3},{3,2},{4,5},{5,4},{6,7},{7,6},{8,9},{9,8},{10,11... | collective-permute-start | bytes 786440 | tf_op jit(solution)/shard_map/ppermute | solution.py:19
  20.6 10.3 %collective-permute-start.5 = (bf16[8,128,128]{2,1,0:T(8,128)(2,1)}, bf16[8,128,128]{2,1,0:T(8,128)(2,1)S(1)}, u32[]{:S(2)}, u32[]{:S(2)}) collective-permute-start(bf16[8,128,128]{2,1,0:T(8,128)(2,1)} %get-tuple-element.22), channel_id=1, source_target_pairs={{0,1},{1,0},{2,3},{3,2},{4,5},{5,4},{6,7},{7,6},{8,9},{9,8},{10,11... | collective-permute-start | bytes 786440 | tf_op jit(solution)/shard_map/ppermute | solution.py:19
  20.7 17.0 %collective-permute-start.7 = (bf16[8,128,128]{2,1,0:T(8,128)(2,1)}, bf16[8,128,128]{2,1,0:T(8,128)(2,1)S(1)}, u32[]{:S(2)}, u32[]{:S(2)}) collective-permute-start(bf16[8,128,128]{2,1,0:T(8,128)(2,1)} %get-tuple-element.24), channel_id=1, source_target_pairs={{0,1},{1,0},{2,3},{3,2},{4,5},{5,4},{6,7},{7,6},{8,9},{9,8},{10,11... | collective-permute-start | bytes 786440 | tf_op jit(solution)/shard_map/ppermute | solution.py:19
  22.6 19.5 %collective-permute-start.9 = (bf16[8,128,128]{2,1,0:T(8,128)(2,1)}, bf16[8,128,128]{2,1,0:T(8,128)(2,1)S(1)}, u32[]{:S(2)}, u32[]{:S(2)}) collective-permute-start(bf16[8,128,128]{2,1,0:T(8,128)(2,1)} %get-tuple-element.25), channel_id=1, source_target_pairs={{0,1},{1,0},{2,3},{3,2},{4,5},{5,4},{6,7},{7,6},{8,9},{9,8},{10,11... | collective-permute-start | bytes 786440 | tf_op jit(solution)/shard_map/ppermute | solution.py:19
  26.3 21.4 %collective-permute-start.4 = (bf16[8,128,128]{2,1,0:T(8,128)(2,1)S(1)}, bf16[8,128,128]{2,1,0:T(8,128)(2,1)S(1)}, u32[]{:S(2)}, u32[]{:S(2)}) collective-permute-start(bf16[8,128,128]{2,1,0:T(8,128)(2,1)S(1)} %add_convert_fusion.3), channel_id=1, source_target_pairs={{0,4},{1,5},{2,6},{3,7},{4,0},{5,1},{6,2},{7,3},{8,12},{9,13},{10,... | collective-permute-start | bytes 786440 | tf_op jit(solution)/shard_map/ppermute | solution.py:19
  31.8 15.8 %collective-permute-start.6 = (bf16[8,128,128]{2,1,0:T(8,128)(2,1)S(1)}, bf16[8,128,128]{2,1,0:T(8,128)(2,1)S(1)}, u32[]{:S(2)}, u32[]{:S(2)}) collective-permute-start(bf16[8,128,128]{2,1,0:T(8,128)(2,1)S(1)} %add_convert_fusion.2), channel_id=1, source_target_pairs={{0,6},{1,7},{2,4},{3,5},{4,2},{5,3},{6,0},{7,1},{8,14},{9,15},{10,... | collective-permute-start | bytes 786440 | tf_op jit(solution)/shard_map/ppermute | solution.py:19
  38.7 15.9 %collective-permute-start.8 = (bf16[8,128,128]{2,1,0:T(8,128)(2,1)S(1)}, bf16[8,128,128]{2,1,0:T(8,128)(2,1)S(1)}, u32[]{:S(2)}, u32[]{:S(2)}) collective-permute-start(bf16[8,128,128]{2,1,0:T(8,128)(2,1)S(1)} %add_convert_fusion.1), channel_id=1, source_target_pairs={{0,2},{1,3},{2,0},{3,1},{4,6},{5,7},{6,4},{7,5},{8,10},{9,11},{10,... | collective-permute-start | bytes 786440 | tf_op jit(solution)/shard_map/ppermute | solution.py:19
  42.1 12.5 %copy-start = (bf16[8,128,128]{2,1,0:T(8,128)(2,1)}, bf16[8,128,128]{2,1,0:T(8,128)(2,1)S(1)}, u32[]{:S(2)}) copy-start(bf16[8,128,128]{2,1,0:T(8,128)(2,1)S(1)} %collective-permute-done.9.refs_4_) | copy-start | bytes 786436
  58.5 48.5 %copy-start.16 = (f32[128,128]{1,0:T(8,128)S(1)}, f32[128,128]{1,0:T(8,128)}, u32[]{:S(2)}) copy-start(f32[128,128]{1,0:T(8,128)} %get-tuple-element.27) | copy-start | bytes 196612
  58.5 11.3 %collective-permute-start.20 = (bf16[8,128,128]{2,1,0:T(8,128)(2,1)}, bf16[8,128,128]{2,1,0:T(8,128)(2,1)S(1)}, u32[]{:S(2)}, u32[]{:S(2)}) collective-permute-start(bf16[8,128,128]{2,1,0:T(8,128)(2,1)} %get-tuple-element.28.refs_5_), channel_id=1, source_target_pairs={{0,6},{1,7},{2,4},{3,5},{4,2},{5,3},{6,0},{7,1},{8,14},{9,15},{10,... | collective-permute-start | bytes 786440 | tf_op jit(solution)/shard_map/ppermute | solution.py:19
  62.3 22.7 %collective-permute-start.18 = (bf16[8,128,128]{2,1,0:T(8,128)(2,1)}, bf16[8,128,128]{2,1,0:T(8,128)(2,1)S(1)}, u32[]{:S(2)}, u32[]{:S(2)}) collective-permute-start(bf16[8,128,128]{2,1,0:T(8,128)(2,1)} %get-tuple-element.28.refs_5_), channel_id=1, source_target_pairs={{0,4},{1,5},{2,6},{3,7},{4,0},{5,1},{6,2},{7,3},{8,12},{9,13},{10,... | collective-permute-start | bytes 786440 | tf_op jit(solution)/shard_map/ppermute | solution.py:19
  62.3 22.7 %collective-permute-start.16 = (bf16[8,128,128]{2,1,0:T(8,128)(2,1)}, bf16[8,128,128]{2,1,0:T(8,128)(2,1)S(1)}, u32[]{:S(2)}, u32[]{:S(2)}) collective-permute-start(bf16[8,128,128]{2,1,0:T(8,128)(2,1)} %get-tuple-element.28.refs_5_), channel_id=1, source_target_pairs={{0,2},{1,3},{2,0},{3,1},{4,6},{5,7},{6,4},{7,5},{8,10},{9,11},{10,... | collective-permute-start | bytes 786440 | tf_op jit(solution)/shard_map/ppermute | solution.py:19
  62.9 24.8 %collective-permute-start.15 = (bf16[8,128,128]{2,1,0:T(8,128)(2,1)}, bf16[8,128,128]{2,1,0:T(8,128)(2,1)S(1)}, u32[]{:S(2)}, u32[]{:S(2)}) collective-permute-start(bf16[8,128,128]{2,1,0:T(8,128)(2,1)} %get-tuple-element.28.refs_5_), channel_id=1, source_target_pairs={{0,1},{1,0},{2,3},{3,2},{4,5},{5,4},{6,7},{7,6},{8,9},{9,8},{10,11... | collective-permute-start | bytes 786440 | tf_op jit(solution)/shard_map/ppermute | solution.py:19
  69.8 28.8 %copy-start.1 = (bf16[8,128,128]{2,1,0:T(8,128)(2,1)}, bf16[8,128,128]{2,1,0:T(8,128)(2,1)S(1)}, u32[]{:S(2)}) copy-start(bf16[8,128,128]{2,1,0:T(8,128)(2,1)S(1)} %collective-permute-done.20.refs_11_) | copy-start | bytes 786436
  69.8 17.9 %collective-permute-start.21 = (bf16[8,128,128]{2,1,0:T(8,128)(2,1)S(1)}, bf16[8,128,128]{2,1,0:T(8,128)(2,1)S(1)}, u32[]{:S(2)}, u32[]{:S(2)}) collective-permute-start(bf16[8,128,128]{2,1,0:T(8,128)(2,1)S(1)} %collective-permute-done.20.refs_11_), channel_id=1, source_target_pairs={{0,1},{1,0},{2,3},{3,2},{4,5},{5,4},{6,7},{7,6},{8,9},{9,8},{10,11... | collective-permute-start | bytes 786440 | tf_op jit(solution)/shard_map/ppermute | solution.py:19
  85.0 13.6 %copy-start.2 = (bf16[8,128,128]{2,1,0:T(8,128)(2,1)}, bf16[8,128,128]{2,1,0:T(8,128)(2,1)S(1)}, u32[]{:S(2)}) copy-start(bf16[8,128,128]{2,1,0:T(8,128)(2,1)S(1)} %collective-permute-done.18.refs_9_) | copy-start | bytes 786436
  85.0 9.2 %collective-permute-start.19 = (bf16[8,128,128]{2,1,0:T(8,128)(2,1)S(1)}, bf16[8,128,128]{2,1,0:T(8,128)(2,1)S(1)}, u32[]{:S(2)}, u32[]{:S(2)}) collective-permute-start(bf16[8,128,128]{2,1,0:T(8,128)(2,1)S(1)} %collective-permute-done.18.refs_9_), channel_id=1, source_target_pairs={{0,1},{1,0},{2,3},{3,2},{4,5},{5,4},{6,7},{7,6},{8,9},{9,8},{10,11... | collective-permute-start | bytes 786440 | tf_op jit(solution)/shard_map/ppermute | solution.py:19
  85.0 13.6 %copy-start.3 = (bf16[8,128,128]{2,1,0:T(8,128)(2,1)}, bf16[8,128,128]{2,1,0:T(8,128)(2,1)S(1)}, u32[]{:S(2)}) copy-start(bf16[8,128,128]{2,1,0:T(8,128)(2,1)S(1)} %collective-permute-done.16.refs_7_) | copy-start | bytes 786436
  85.0 13.5 %collective-permute-start.17 = (bf16[8,128,128]{2,1,0:T(8,128)(2,1)S(1)}, bf16[8,128,128]{2,1,0:T(8,128)(2,1)S(1)}, u32[]{:S(2)}, u32[]{:S(2)}) collective-permute-start(bf16[8,128,128]{2,1,0:T(8,128)(2,1)S(1)} %collective-permute-done.16.refs_7_), channel_id=1, source_target_pairs={{0,1},{1,0},{2,3},{3,2},{4,5},{5,4},{6,7},{7,6},{8,9},{9,8},{10,11... | collective-permute-start | bytes 786440 | tf_op jit(solution)/shard_map/ppermute | solution.py:19
  87.7 10.9 %copy-start.4 = (bf16[8,128,128]{2,1,0:T(8,128)(2,1)}, bf16[8,128,128]{2,1,0:T(8,128)(2,1)S(1)}, u32[]{:S(2)}) copy-start(bf16[8,128,128]{2,1,0:T(8,128)(2,1)S(1)} %collective-permute-done.15.refs_6_) | copy-start | bytes 786436
  87.7 10.9 %copy-start.6 = (bf16[8,128,128]{2,1,0:T(8,128)(2,1)}, bf16[8,128,128]{2,1,0:T(8,128)(2,1)S(1)}, u32[]{:S(2)}) copy-start(bf16[8,128,128]{2,1,0:T(8,128)(2,1)S(1)} %collective-permute-done.21.refs_12_) | copy-start | bytes 786436
  104.9 4.0 %collective-permute-start.22 = (bf16[8,128,128]{2,1,0:T(8,128)(2,1)}, bf16[8,128,128]{2,1,0:T(8,128)(2,1)S(1)}, u32[]{:S(2)}, u32[]{:S(2)}) collective-permute-start(bf16[8,128,128]{2,1,0:T(8,128)(2,1)} %get-tuple-element.31), channel_id=1, source_target_pairs={{0,8},{8,0},{16,24},{24,16},{1,9},{9,1},{17,25},{25,17},{2,10},{10... | collective-permute-start | bytes 786440 | tf_op jit(solution)/shard_map/ppermute | solution.py:19
  107.0 1.5 %collective-permute-start.10 = (f32[128,128]{1,0:T(8,128)S(1)}, f32[128,128]{1,0:T(8,128)S(1)}, u32[]{:S(2)}, u32[]{:S(2)}) collective-permute-start(f32[128,128]{1,0:T(8,128)S(1)} %copy-done.16), channel_id=1, source_target_pairs={{0,8},{8,0},{16,24},{24,16},{1,9},{9,1},{17,25},{25,17},{2,10},{10... | collective-permute-start | bytes 196616 | tf_op jit(solution)/shard_map/ppermute | solution.py:19
  108.4 4.4 %collective-permute-start.11 = (f32[128,128]{1,0:T(8,128)S(1)}, f32[128,128]{1,0:T(8,128)S(1)}, u32[]{:S(2)}, u32[]{:S(2)}) collective-permute-start(f32[128,128]{1,0:T(8,128)S(1)} %add.30), channel_id=1, source_target_pairs={{0,16},{8,24},{16,0},{24,8},{1,17},{9,25},{17,1},{25,9},{2,18},{10... | collective-permute-start | bytes 196616 | tf_op jit(solution)/shard_map/ppermute | solution.py:19
  108.5 19.6 %collective-permute-start.24 = (bf16[8,128,128]{2,1,0:T(8,128)(2,1)}, bf16[8,128,128]{2,1,0:T(8,128)(2,1)S(1)}, u32[]{:S(2)}, u32[]{:S(2)}) collective-permute-start(bf16[8,128,128]{2,1,0:T(8,128)(2,1)} %get-tuple-element.32), channel_id=1, source_target_pairs={{0,8},{8,0},{16,24},{24,16},{1,9},{9,1},{17,25},{25,17},{2,10},{10... | collective-permute-start | bytes 786440 | tf_op jit(solution)/shard_map/ppermute | solution.py:19
  110.0 18.2 %collective-permute-start.23 = (bf16[8,128,128]{2,1,0:T(8,128)(2,1)S(1)}, bf16[8,128,128]{2,1,0:T(8,128)(2,1)S(1)}, u32[]{:S(2)}, u32[]{:S(2)}) collective-permute-start(bf16[8,128,128]{2,1,0:T(8,128)(2,1)S(1)} %add_convert_fusion), channel_id=1, source_target_pairs={{0,16},{8,24},{16,0},{24,8},{1,17},{9,25},{17,1},{25,9},{2,18},{10... | collective-permute-start | bytes 786440 | tf_op jit(solution)/shard_map/ppermute | solution.py:19
  112.9 4.3 %collective-permute-start.12 = (f32[128,128]{1,0:T(8,128)S(1)}, f32[128,128]{1,0:T(8,128)S(1)}, u32[]{:S(2)}, u32[]{:S(2)}) collective-permute-start(f32[128,128]{1,0:T(8,128)S(1)} %add.31), channel_id=1, source_target_pairs={{0,1},{1,0},{2,3},{3,2},{4,5},{5,4},{6,7},{7,6},{8,9},{9,8},{10,11... | collective-permute-start | bytes 196616 | tf_op jit(solution)/shard_map/ppermute | solution.py:19
  117.2 4.3 %collective-permute-start.13 = (f32[128,128]{1,0:T(8,128)S(1)}, f32[128,128]{1,0:T(8,128)S(1)}, u32[]{:S(2)}, u32[]{:S(2)}) collective-permute-start(f32[128,128]{1,0:T(8,128)S(1)} %add.32), channel_id=1, source_target_pairs={{0,2},{1,3},{2,0},{3,1},{4,6},{5,7},{6,4},{7,5},{8,10},{9,11},{10,... | collective-permute-start | bytes 196616 | tf_op jit(solution)/shard_map/ppermute | solution.py:19
  121.6 5.9 %collective-permute-start.14 = (f32[128,128]{1,0:T(8,128)S(1)}, f32[128,128]{1,0:T(8,128)S(1)}, u32[]{:S(2)}, u32[]{:S(2)}) collective-permute-start(f32[128,128]{1,0:T(8,128)S(1)} %add.33), channel_id=1, source_target_pairs={{0,4},{1,5},{2,6},{3,7},{4,0},{5,1},{6,2},{7,3},{8,12},{9,13},{10,... | collective-permute-start | bytes 196616 | tf_op jit(solution)/shard_map/ppermute | solution.py:19
  (10 other events, 24.2 us)

commit v2 on v1

--- a/solution.py
+++ b/solution.py
@@ -19,27 +19,65 @@
     return lax.ppermute(value, axis, [(i, i ^ mask) for i in range(size)])
 
 
+def is_inner(index):
+    return (index // 2) % 4 in (1, 2)
+
+
+def permute_some(value, axis, mask, keep):
+    size = lax.axis_size(axis)
+    return lax.ppermute(value, axis, [(i, i ^ mask) for i in range(size) if keep(i)])
+
+
+def is_outer(index):
+    return not is_inner(index)
+
+
 def gather_pieces(value, axis):
     size = lax.axis_size(axis)
     pieces = [None] * size
-    pieces[0] = value
-    for major in list(range(4, size, 2)) + [2]:
-        if major < size:
-            pieces[major] = permute_xor(value, axis, major)
-    for major in [0] + list(range(4, size, 2)) + [2]:
-        if major < size:
-            pieces[major + 1] = permute_xor(pieces[major], axis, 1)
+    pieces[0] = [value]
+    if size == 8:
+        pieces[4] = [permute_xor(value, axis, 4)]
+        inner = permute_some(value, axis, 6, is_inner)
+        pieces[2] = [permute_xor(value, axis, 2)]
+        pieces[1] = [permute_xor(value, axis, 1)]
+        outer = permute_some(pieces[4][0], axis, 2, is_inner)
+        pieces[5] = [permute_xor(pieces[4][0], axis, 1)]
+        pieces[3] = [permute_xor(pieces[2][0], axis, 1)]
+        pieces[6] = [inner, outer]
+        pieces[7] = [
+            permute_some(inner, axis, 1, is_inner),
+            permute_some(outer, axis, 1, is_outer),
+        ]
+        return pieces
+    for major in range(2, size, 2):
+        pieces[major] = [permute_xor(value, axis, major)]
+    for major in range(0, size, 2):
+        pieces[major + 1] = [permute_xor(pieces[major][0], axis, 1)]
     return pieces
+
+
+def join(*values):
+    total = values[0].astype(F32)
+    for value in values[1:]:
+        total = total + value.astype(F32)
+    return total.astype(BF16)
 
 
 def scatter_pieces(parts, axis):
     size = len(parts)
+    if size == 8:
+        received = {r: permute_xor(parts[r], axis, 1) for r in (7, 5, 3, 1)}
+        far = join(parts[6], received[7])
+        outer = permute_some(far, axis, 2, is_outer)
+        inner = permute_some(far, axis, 6, is_inner)
+        skip = permute_xor(join(parts[4], received[5], outer), axis, 4)
+        near = permute_xor(join(parts[2], received[3]), axis, 2)
+        return [parts[0], received[1], inner, skip, near]
     terms = [parts[0]]
-    for major in list(range(4, size, 2)) + [2]:
-        if major < size:
-            received = permute_xor(parts[major + 1], axis, 1)
-            joined = (parts[major].astype(F32) + received.astype(F32)).astype(BF16)
-            terms.append(permute_xor(joined, axis, major))
+    for major in range(2, size, 2):
+        received = permute_xor(parts[major + 1], axis, 1)
+        terms.append(permute_xor(join(parts[major], received), axis, major))
     terms.append(permute_xor(parts[1], axis, 1))
     return terms
 
@@ -53,20 +91,29 @@
     return value
 
 
-def tile_kernel(n_src, n_out, tile_size, slots, to_rows, *refs):
+def tile_kernel(choices, n_out, slots, to_rows, *refs):
+    n_src = len(choices)
+    n_arrays = sum(choices)
     rows_ref, cols_ref, count_ref, ids_ref, adj_hbm = refs[:5]
-    sources = refs[5 : 5 + n_src]
-    outs = refs[5 + n_src : 5 + n_src + n_out]
-    adj, source, acc, sems = refs[5 + n_src + n_out :]
+    arrays = list(refs[5 : 5 + n_arrays])
+    outs = refs[5 + n_arrays : 5 + n_arrays + n_out]
+    adj, source, acc, sems = refs[5 + n_arrays + n_out :]
     src_id = ids_ref[0]
     out_id = ids_ref[1]
     adj_copy = pltpu.make_async_copy(adj_hbm, adj, sems.at[n_src])
     adj_copy.start()
     copies = []
-    for r in range(n_src):
-        copy = pltpu.make_async_copy(sources[r], source.at[src_id ^ r], sems.at[r])
-        copy.start()
-        copies.append(copy)
+    for r, choice in enumerate(choices):
+        options = [
+            pltpu.make_async_copy(arrays.pop(0), source.at[src_id ^ r], sems.at[r])
+            for _ in range(choice)
+        ]
+        if choice == 1:
+            options[0].start()
+        else:
+            pl.when(ids_ref[2] == 1)(options[0].start)
+            pl.when(ids_ref[2] == 0)(options[1].start)
+        copies.append(options[0])
     out_tiles = n_out * outs[0].shape[0]
     src_tiles = source.shape[1]
     acc[...] = jnp.zeros(acc.shape, F32)
@@ -104,14 +151,15 @@
 def tile_pass(rows, cols, count, ids, adj_tiles, pieces, n_out, out_tiles, to_rows):
     slots, tile_size, _ = adj_tiles.shape
     n_src = len(pieces)
-    block = pieces[0].shape
+    arrays = [array for piece in pieces for array in piece]
+    block = arrays[0].shape
     width = block[-1]
     smem = pl.BlockSpec(memory_space=pltpu.SMEM)
     hbm = pl.BlockSpec(memory_space=pl.ANY)
     vmem = pl.BlockSpec(memory_space=pltpu.VMEM)
     return pl.pallas_call(
-        functools.partial(tile_kernel, n_src, n_out, tile_size, slots, to_rows),
-        in_specs=[smem] * 4 + [hbm] * (1 + n_src),
+        functools.partial(tile_kernel, [len(piece) for piece in pieces], n_out, slots, to_rows),
+        in_specs=[smem] * 4 + [hbm] * (1 + len(arrays)),
         out_specs=[vmem] * n_out,
         out_shape=[jax.ShapeDtypeStruct((out_tiles, tile_size, width), BF16)] * n_out,
         scratch_shapes=[
@@ -120,7 +168,7 @@
             pltpu.VMEM((n_out * out_tiles + 1, tile_size, width), F32),
             pltpu.SemaphoreType.DMA((n_src + 1,)),
         ],
-    )(rows, cols, count, ids, adj_tiles, *pieces)
+    )(rows, cols, count, ids, adj_tiles, *arrays)
 
 
 def middle_kernel(n_terms, *refs):
@@ -186,17 +234,20 @@
     as_tiles = (dev_tiles, tile_size, width)
     row_id = lax.axis_index("row").astype(jnp.int32)
     col_id = lax.axis_index("col").astype(jnp.int32)
+    inner = ((col_id // 2) % 4 == 1) | ((col_id // 2) % 4 == 2)
+    inner = inner.astype(jnp.int32)
     table = (tile_rows, tile_cols, tile_count)
     group = gather_pieces(features.reshape(as_tiles), "row")
     parts = tile_pass(
-        *table, jnp.stack([row_id, col_id]), adj_tiles, group, lax.axis_size("col"), dev_tiles, True
+        *table, jnp.stack([row_id, col_id, inner]), adj_tiles, group, lax.axis_size("col"), dev_tiles, True
     )
     terms = scatter_pieces(parts, "col")
     out_features, grad, wterm = middle(terms, weight, cotangent.reshape(as_tiles))
     panel = gather_pieces(grad, "col")
     weight_grad = all_sum(wterm, ("row", "col"))
+    panel, weight_grad = lax.optimization_barrier((panel, weight_grad))
     parts = tile_pass(
-        *table, jnp.stack([col_id, row_id]), adj_tiles, panel, lax.axis_size("row"), dev_tiles, False
+        *table, jnp.stack([col_id, row_id, inner]), adj_tiles, panel, lax.axis_size("row"), dev_tiles, False
     )
     feature_grad = final(scatter_pieces(parts, "row"))
     return (

time: 131 us -> 133 us (1.015)
  waiting for transfers between devices: 69.3 us -> 62 us
  starting transfers between devices: 34.3 us -> 39.7 us
  Pallas kernels: 16.5 us -> 18.4 us
    ppermute x25 -> x22, waiting for transfers between devices: 69.3 us -> 58.4 us  [permute_xor(): return lax.ppermute(value, axis, [(i, i ^ mask) for i in range(size)])]
    ppermute x0 -> x6, starting transfers between devices: none -> 9.1 us  [permute_some(): lax.ppermute(value, axis, [(i, i ^ mask) for i in range(size) if keep(i)])]
    ppermute x25 -> x22, starting transfers between devices: 34.3 us -> 30.6 us  [permute_xor(): return lax.ppermute(value, axis, [(i, i ^ mask) for i in range(size)])]
    ppermute x0 -> x6, waiting for transfers between devices: none -> 3.58 us  [permute_some(): lax.ppermute(value, axis, [(i, i ^ mask) for i in range(size) if keep(i)])]
    pallas_call x2, Pallas kernels: 11.3 us -> 13.2 us  [tile_pass(): pl.pallas_call(functools.partial(tile_kernel, [len(piece) for piece in pi...]
    unnamed x34 -> x36, local copies, waits for them, and re-layouts: 3.36 us -> 3.27 us
  transfers between devices with their start and end apart: 25 -> 28, of which waited for: 16 -> 17; matrix products, arithmetic and copies ran while one was open for 5% -> 5% of each run, Pallas kernels for 0% -> 0%
where the time goes in v2:
time: 133 us; the launch traced here: 132 us
  waiting for transfers between devices  62 us (47%)
  starting transfers between devices  39.7 us (30%)
  Pallas kernels  18.4 us (14%)
  other arithmetic  6.86 us (5%)
  local copies, waits for them, and re-layouts  3.27 us (2%)
  between operations  1.51 us (1%)
    ppermute x22, waiting for transfers between devices, permute_xor(): return lax.ppermute(value, axis, [(i, i ^ mask) for i in range(size)])  58.4 us
    ppermute x22, starting transfers between devices, permute_xor(): return lax.ppermute(value, axis, [(i, i ^ mask) for i in range(size)])  30.6 us
    pallas_call x2, Pallas kernels, tile_pass(): pl.pallas_call(functools.partial(tile_kernel, [len(piece) for piece in pi...  13.2 us
    ppermute x6, starting transfers between devices, permute_some(): lax.ppermute(value, axis, [(i, i ^ mask) for i in range(size) if keep(i)])  9.1 us
    convert_element_type x4, other arithmetic, join(): return total.astype(BF16)  4.13 us
    ppermute x6, waiting for transfers between devices, permute_some(): lax.ppermute(value, axis, [(i, i ^ mask) for i in range(size) if keep(i)])  3.58 us
    unnamed x36, local copies, waits for them, and re-layouts  3.27 us
    pallas_call x1, Pallas kernels, middle(): pl.pallas_call(functools.partial(middle_kernel, len(terms)), out_shape=[j...  3.2 us
  transfers between devices with their start and end apart: 28, of which 17 were waited for; matrix products, arithmetic and copies ran while one was open for 5% of the time, Pallas kernels for 0%

profile of v2, /device:TPU:0, one launch (start us, length us, event | category | flops | bytes accessed | tf_op | source)
XLA Modules:
  0.0 131.7 jit_solution(14397348713772237353)
XLA Ops:
  0.6 3.1 %collective-permute-start.1 = (bf16[8,128,128]{2,1,0:T(8,128)(2,1)}, bf16[8,128,128]{2,1,0:T(8,128)(2,1)S(1)}, u32[]{:S(2)}, u32[]{:S(2)}) collective-permute-start(bf16[8,128,128]{2,1,0:T(8,128)(2,1)} %bitcast.9), channel_id=1, source_target_pairs={{0,16},{8,24},{16,0},{24,8},{1,17},{9,25},{17,1},{25,9},{2,18},{10... | collective-permute-start | bytes 786440 | tf_op jit(solution)/shard_map/ppermute | solution.py:19
  3.7 6.5 %collective-permute-done.1.refs_7_ = bf16[8,128,128]{2,1,0:T(8,128)(2,1)S(1)} collective-permute-done((bf16[8,128,128]{2,1,0:T(8,128)(2,1)}, bf16[8,128,128]{2,1,0:T(8,128)(2,1)S(1)}, u32[]{:S(2)}, u32[]{:S(2)}) %collective-permute-start.1) | collective-permute-done | bytes 262176 | tf_op jit(solution)/shard_map/ppermute | solution.py:19
  12.9 6.7 %shard_map.94 = (bf16[8,128,128]{2,1,0:T(8,128)(2,1)}, bf16[8,128,128]{2,1,0:T(8,128)(2,1)}, bf16[8,128,128]{2,1,0:T(8,128)(2,1)}, bf16[8,128,128]{2,1,0:T(8,128...) custom-call(s32[96]{0:T(128)} %refs_0_.3, ...), custom_call_target="tpu_custom_call" | custom-call | tf_op jit(solution)/shard_map/pallas_call | solution.py:160
  22.6 6.4 %collective-permute-done.4 = bf16[8,128,128]{2,1,0:T(8,128)(2,1)S(1)} collective-permute-done((bf16[8,128,128]{2,1,0:T(8,128)(2,1)}, bf16[8,128,128]{2,1,0:T(8,128)(2,1)S(1)}, u32[]{:S(2)}, u32[]{:S(2)}) %collective-permute-start.4) | collective-permute-done | bytes 262176 | tf_op jit(solution)/shard_map/ppermute | solution.py:19
  30.1 3.2 %collective-permute-start.7 = (bf16[8,128,128]{2,1,0:T(8,128)(2,1)S(1)}, bf16[8,128,128]{2,1,0:T(8,128)(2,1)S(1)}, u32[]{:S(2)}, u32[]{:S(2)}) collective-permute-start(bf16[8,128,128]{2,1,0:T(8,128)(2,1)S(1)} %add_convert_fusion.3), channel_id=1, source_target_pairs={{0,2},{1,3},{6,4},{7,5},{8,10},{9,11},{14,12},{15,13},{16,18},{17,... | collective-permute-start | bytes 786440 | tf_op jit(solution)/shard_map/ppermute | solution.py:28
  33.3 2.1 %collective-permute-start.3 = (bf16[8,128,128]{2,1,0:T(8,128)(2,1)}, bf16[8,128,128]{2,1,0:T(8,128)(2,1)S(1)}, u32[]{:S(2)}, u32[]{:S(2)}) collective-permute-start(bf16[8,128,128]{2,1,0:T(8,128)(2,1)} %get-tuple-element.30), channel_id=1, source_target_pairs={{0,1},{1,0},{2,3},{3,2},{4,5},{5,4},{6,7},{7,6},{8,9},{9,8},{10,11... | collective-permute-start | bytes 786440 | tf_op jit(solution)/shard_map/ppermute | solution.py:19
  37.1 2.0 %collective-permute-start.10 = (bf16[8,128,128]{2,1,0:T(8,128)(2,1)S(1)}, bf16[8,128,128]{2,1,0:T(8,128)(2,1)S(1)}, u32[]{:S(2)}, u32[]{:S(2)}) collective-permute-start(bf16[8,128,128]{2,1,0:T(8,128)(2,1)S(1)} %add_convert_fusion.1), channel_id=1, source_target_pairs={{0,2},{1,3},{2,0},{3,1},{4,6},{5,7},{6,4},{7,5},{8,10},{9,11},{10,... | collective-permute-start | bytes 786440 | tf_op jit(solution)/shard_map/ppermute | solution.py:19
  41.3 2.9 %collective-permute-start.8 = (bf16[8,128,128]{2,1,0:T(8,128)(2,1)S(1)}, bf16[8,128,128]{2,1,0:T(8,128)(2,1)S(1)}, u32[]{:S(2)}, u32[]{:S(2)}) collective-permute-start(bf16[8,128,128]{2,1,0:T(8,128)(2,1)S(1)} %add_convert_fusion.2), channel_id=1, source_target_pairs={{0,4},{1,5},{2,6},{3,7},{4,0},{5,1},{6,2},{7,3},{8,12},{9,13},{10,... | collective-permute-start | bytes 786440 | tf_op jit(solution)/shard_map/ppermute | solution.py:19
  44.2 1.2 collective-permute-done.3.refs_1_
  45.8 9.6 %collective-permute-done.8.refs_3_ = bf16[8,128,128]{2,1,0:T(8,128)(2,1)S(1)} collective-permute-done((bf16[8,128,128]{2,1,0:T(8,128)(2,1)S(1)}, bf16[8,128,128]{2,1,0:T(8,128)(2,1)S(1)}, u32[]{:S(2)}, u32[]{:S(2)}) %collective-permute-start.8) | collective-permute-done | bytes 262176 | tf_op jit(solution)/shard_map/ppermute | solution.py:19
  56.1 3.2 %shard_map.95 = (bf16[8,128,128]{2,1,0:T(8,128)(2,1)}, bf16[8,128,128]{2,1,0:T(8,128)(2,1)}, f32[128,128]{1,0:T(8,128)}) custom-call(bf16[8,128,128]{2,1,0:T(8,128)(2,1)} %get-tuple-element.29.refs_0_, bf16[8,128,128]{2,1,0:T(8,128)(2,1)} %copy-done, bf16[8,128,128]{2,1,0:T(8,128)(2,1)} %copy-done.1, bf16[8,128,128]{2,1,0:T(8,128)(2,1)} %copy-done.3, ...), custom_call_target="tpu_custom_call" | custom-call | tf_op jit(solution)/shard_map/pallas_call | solution.py:204
  59.3 1.5 %collective-permute-done.20 = f32[128,128]{1,0:T(8,128)S(1)} collective-permute-done((f32[128,128]{1,0:T(8,128)}, f32[128,128]{1,0:T(8,128)S(1)}, u32[]{:S(2)}, u32[]{:S(2)}) %collective-permute-start.20) | collective-permute-done | bytes 65568 | tf_op jit(solution)/shard_map/ppermute | solution.py:19
  61.6 1.8 %collective-permute-start.21 = (f32[128,128]{1,0:T(8,128)S(1)}, f32[128,128]{1,0:T(8,128)S(1)}, u32[]{:S(2)}, u32[]{:S(2)}) collective-permute-start(f32[128,128]{1,0:T(8,128)S(1)} %add.41), channel_id=1, source_target_pairs={{0,16},{8,24},{16,0},{24,8},{1,17},{9,25},{17,1},{25,9},{2,18},{10... | collective-permute-start | bytes 196616 | tf_op jit(solution)/shard_map/ppermute | solution.py:19
  64.1 4.8 %collective-permute-start.12 = (bf16[8,128,128]{2,1,0:T(8,128)(2,1)}, bf16[8,128,128]{2,1,0:T(8,128)(2,1)S(1)}, u32[]{:S(2)}, u32[]{:S(2)}) collective-permute-start(bf16[8,128,128]{2,1,0:T(8,128)(2,1)} %get-tuple-element.41.refs_5_), channel_id=1, source_target_pairs={{0,2},{1,3},{2,0},{3,1},{4,6},{5,7},{6,4},{7,5},{8,10},{9,11},{10,... | collective-permute-start | bytes 786440 | tf_op jit(solution)/shard_map/ppermute | solution.py:19
  68.9 5.6 %collective-permute-done.14.refs_9_ = bf16[8,128,128]{2,1,0:T(8,128)(2,1)S(1)} collective-permute-done((bf16[8,128,128]{2,1,0:T(8,128)(2,1)}, bf16[8,128,128]{2,1,0:T(8,128)(2,1)S(1)}, u32[]{:S(2)}, u32[]{:S(2)}) %collective-permute-start.14) | collective-permute-done | bytes 262176 | tf_op jit(solution)/shard_map/ppermute | solution.py:19
  74.5 1.3 collective-permute-start.17
  75.8 1.7 %collective-permute-start.22 = (f32[128,128]{1,0:T(8,128)S(1)}, f32[128,128]{1,0:T(8,128)S(1)}, u32[]{:S(2)}, u32[]{:S(2)}) collective-permute-start(f32[128,128]{1,0:T(8,128)S(1)} %add.42), channel_id=1, source_target_pairs={{0,1},{1,0},{2,3},{3,2},{4,5},{5,4},{6,7},{7,6},{8,9},{9,8},{10,11... | collective-permute-start | bytes 196616 | tf_op jit(solution)/shard_map/ppermute | solution.py:19
  77.5 2.6 %collective-permute-done.22 = f32[128,128]{1,0:T(8,128)S(1)} collective-permute-done((f32[128,128]{1,0:T(8,128)S(1)}, f32[128,128]{1,0:T(8,128)S(1)}, u32[]{:S(2)}, u32[]{:S(2)}) %collective-permute-start.22) | collective-permute-done | bytes 65568 | tf_op jit(solution)/shard_map/ppermute | solution.py:19
  80.2 2.7 %collective-permute-start.23 = (f32[128,128]{1,0:T(8,128)S(1)}, f32[128,128]{1,0:T(8,128)S(1)}, u32[]{:S(2)}, u32[]{:S(2)}) collective-permute-start(f32[128,128]{1,0:T(8,128)S(1)} %add.43), channel_id=1, source_target_pairs={{0,2},{1,3},{2,0},{3,1},{4,6},{5,7},{6,4},{7,5},{8,10},{9,11},{10,... | collective-permute-start | bytes 196616 | tf_op jit(solution)/shard_map/ppermute | solution.py:19
  82.9 2.6 %collective-permute-done.23 = f32[128,128]{1,0:T(8,128)S(1)} collective-permute-done((f32[128,128]{1,0:T(8,128)S(1)}, f32[128,128]{1,0:T(8,128)S(1)}, u32[]{:S(2)}, u32[]{:S(2)}) %collective-permute-start.23) | collective-permute-done | bytes 65568 | tf_op jit(solution)/shard_map/ppermute | solution.py:19
  85.6 1.4 %collective-permute-start.11 = (bf16[8,128,128]{2,1,0:T(8,128)(2,1)}, bf16[8,128,128]{2,1,0:T(8,128)(2,1)S(1)}, u32[]{:S(2)}, u32[]{:S(2)}) collective-permute-start(bf16[8,128,128]{2,1,0:T(8,128)(2,1)} %get-tuple-element.41.refs_5_), channel_id=1, source_target_pairs={{0,1},{1,0},{2,3},{3,2},{4,5},{5,4},{6,7},{7,6},{8,9},{9,8},{10,11... | collective-permute-start | bytes 786440 | tf_op jit(solution)/shard_map/ppermute | solution.py:19
  88.4 2.4 %collective-permute-done.24 = f32[128,128]{1,0:T(8,128)S(1)} collective-permute-done((f32[128,128]{1,0:T(8,128)S(1)}, f32[128,128]{1,0:T(8,128)S(1)}, u32[]{:S(2)}, u32[]{:S(2)}) %collective-permute-start.24) | collective-permute-done | bytes 65568 | tf_op jit(solution)/shard_map/ppermute | solution.py:19
  90.7 1.3 collective-permute-start.13
  92.0 2.6 %collective-permute-start.19 = (bf16[8,128,128]{2,1,0:T(8,128)(2,1)S(1)}, bf16[8,128,128]{2,1,0:T(8,128)(2,1)S(1)}, u32[]{:S(2)}, u32[]{:S(2)}) collective-permute-start(bf16[8,128,128]{2,1,0:T(8,128)(2,1)S(1)} %collective-permute-done.17.refs_12_), channel_id=1, source_target_pairs={{0,1},{1,0},{6,7},{7,6},{8,9},{9,8},{14,15},{15,14},{16,17},{17,16... | collective-permute-start | bytes 786440 | tf_op jit(solution)/shard_map/ppermute | solution.py:28
  96.0 4.7 %collective-permute-done.15.refs_10_ = bf16[8,128,128]{2,1,0:T(8,128)(2,1)S(1)} collective-permute-done((bf16[8,128,128]{2,1,0:T(8,128)(2,1)S(1)}, bf16[8,128,128]{2,1,0:T(8,128)(2,1)S(1)}, u32[]{:S(2)}, u32[]{:S(2)}) %collective-permute-start.15) | collective-permute-done | bytes 262176 | tf_op jit(solution)/shard_map/ppermute | solution.py:19
  100.7 5.6 %collective-permute-done.13.refs_8_ = bf16[8,128,128]{2,1,0:T(8,128)(2,1)S(1)} collective-permute-done((bf16[8,128,128]{2,1,0:T(8,128)(2,1)S(1)}, bf16[8,128,128]{2,1,0:T(8,128)(2,1)S(1)}, u32[]{:S(2)}, u32[]{:S(2)}) %collective-permute-start.13) | collective-permute-done | bytes 262176 | tf_op jit(solution)/shard_map/ppermute | solution.py:19
  106.3 3.6 %collective-permute-done.19.refs_14_ = bf16[8,128,128]{2,1,0:T(8,128)(2,1)S(1)} collective-permute-done((bf16[8,128,128]{2,1,0:T(8,128)(2,1)S(1)}, bf16[8,128,128]{2,1,0:T(8,128)(2,1)S(1)}, u32[]{:S(2)}, u32[]{:S(2)}) %collective-permute-start.19) | collective-permute-done | bytes 262176 | tf_op jit(solution)/shard_map/ppermute | solution.py:28
  110.6 6.5 %shard_map.96 = (bf16[8,128,128]{2,1,0:T(8,128)(2,1)}, bf16[8,128,128]{2,1,0:T(8,128)(2,1)}, bf16[8,128,128]{2,1,0:T(8,128)(2,1)}, bf16[8,128,128]{2,1,0:T(8,128)(2,1)}) custom-call(s32[96]{0:T(128)} %refs_0_.3, s32[96]{0:T(128)} %refs_1_.3, s32[1]{0:T(128)S(6)} %copy.10.refs_2_, s32[3]{0:T(128)} %add_add_fusion.1.refs_3_, bf16[96,128,128]{2,1,0:T(8,128)(2,1)} %refs_4_.3, ...), custom_call_target="tpu_custom_call" | custom-call | tf_op jit(solution)/shard_map/pallas_call | solution.py:160
  117.7 1.2 collective-permute-done.25
  120.0 2.4 %collective-permute-start.26 = (bf16[8,128,128]{2,1,0:T(8,128)(2,1)S(1)}, bf16[8,128,128]{2,1,0:T(8,128)(2,1)S(1)}, u32[]{:S(2)}, u32[]{:S(2)}) collective-permute-start(bf16[8,128,128]{2,1,0:T(8,128)(2,1)S(1)} %add_convert_fusion), channel_id=1, source_target_pairs={{0,16},{8,24},{16,0},{24,8},{1,17},{9,25},{17,1},{25,9},{2,18},{10... | collective-permute-start | bytes 786440 | tf_op jit(solution)/shard_map/ppermute | solution.py:19
  122.4 6.6 %collective-permute-done.26.refs_1_ = bf16[8,128,128]{2,1,0:T(8,128)(2,1)S(1)} collective-permute-done((bf16[8,128,128]{2,1,0:T(8,128)(2,1)S(1)}, bf16[8,128,128]{2,1,0:T(8,128)(2,1)S(1)}, u32[]{:S(2)}, u32[]{:S(2)}) %collective-permute-start.26) | collective-permute-done | bytes 262176 | tf_op jit(solution)/shard_map/ppermute | solution.py:19
  129.7 2.0 %shard_map.97 = bf16[8,128,128]{2,1,0:T(8,128)(2,1)} custom-call(bf16[8,128,128]{2,1,0:T(8,128)(2,1)} %get-tuple-element.51.refs_0_, bf16[8,128,128]{2,1,0:T(8,128)(2,1)} %copy-done.5, bf16[8,128,128]{2,1,0:T(8,128)(2,1)} %copy-done.4), custom_call_target="tpu_custom_call" | custom-call | tf_op jit(solution)/shard_map/pallas_call | solution.py:224
  (75 shorter events, 18.4 us)
Async XLA Ops:
  0.6 9.6 %collective-permute-start.1 = (bf16[8,128,128]{2,1,0:T(8,128)(2,1)}, bf16[8,128,128]{2,1,0:T(8,128)(2,1)S(1)}, u32[]{:S(2)}, u32[]{:S(2)}) collective-permute-start(bf16[8,128,128]{2,1,0:T(8,128)(2,1)} %bitcast.9), channel_id=1, source_target_pairs={{0,16},{8,24},{16,0},{24,8},{1,17},{9,25},{17,1},{25,9},{2,18},{10... | collective-permute-start | bytes 786440 | tf_op jit(solution)/shard_map/ppermute | solution.py:19
  3.7 7.8 %collective-permute-start = (bf16[8,128,128]{2,1,0:T(8,128)(2,1)}, bf16[8,128,128]{2,1,0:T(8,128)(2,1)S(1)}, u32[]{:S(2)}, u32[]{:S(2)}) collective-permute-start(bf16[8,128,128]{2,1,0:T(8,128)(2,1)} %bitcast.10), channel_id=1, source_target_pairs={{0,8},{8,0},{16,24},{24,16},{1,9},{9,1},{17,25},{25,17},{2,10},{10... | collective-permute-start | bytes 786440 | tf_op jit(solution)/shard_map/ppermute | solution.py:19
  10.2 1.5 %collective-permute-start.2 = (bf16[8,128,128]{2,1,0:T(8,128)(2,1)S(1)}, bf16[8,128,128]{2,1,0:T(8,128)(2,1)S(1)}, u32[]{:S(2)}, u32[]{:S(2)}) collective-permute-start(bf16[8,128,128]{2,1,0:T(8,128)(2,1)S(1)} %collective-permute-done.1.refs_7_), channel_id=1, source_target_pairs={{0,8},{8,0},{16,24},{24,16},{1,9},{9,1},{17,25},{25,17},{2,10},{10... | collective-permute-start | bytes 786440 | tf_op jit(solution)/shard_map/ppermute | solution.py:19
  19.6 9.5 %collective-permute-start.4 = (bf16[8,128,128]{2,1,0:T(8,128)(2,1)}, bf16[8,128,128]{2,1,0:T(8,128)(2,1)S(1)}, u32[]{:S(2)}, u32[]{:S(2)}) collective-permute-start(bf16[8,128,128]{2,1,0:T(8,128)(2,1)} %get-tuple-element.32), channel_id=1, source_target_pairs={{0,1},{1,0},{2,3},{3,2},{4,5},{5,4},{6,7},{7,6},{8,9},{9,8},{10,11... | collective-permute-start | bytes 786440 | tf_op jit(solution)/shard_map/ppermute | solution.py:19
  20.6 15.4 %collective-permute-start.9 = (bf16[8,128,128]{2,1,0:T(8,128)(2,1)}, bf16[8,128,128]{2,1,0:T(8,128)(2,1)S(1)}, u32[]{:S(2)}, u32[]{:S(2)}) collective-permute-start(bf16[8,128,128]{2,1,0:T(8,128)(2,1)} %get-tuple-element.36), channel_id=1, source_target_pairs={{0,1},{1,0},{2,3},{3,2},{4,5},{5,4},{6,7},{7,6},{8,9},{9,8},{10,11... | collective-permute-start | bytes 786440 | tf_op jit(solution)/shard_map/ppermute | solution.py:19
  21.7 18.6 %collective-permute-start.6 = (bf16[8,128,128]{2,1,0:T(8,128)(2,1)}, bf16[8,128,128]{2,1,0:T(8,128)(2,1)S(1)}, u32[]{:S(2)}, u32[]{:S(2)}) collective-permute-start(bf16[8,128,128]{2,1,0:T(8,128)(2,1)} %get-tuple-element.34), channel_id=1, source_target_pairs={{0,1},{1,0},{2,3},{3,2},{4,5},{5,4},{6,7},{7,6},{8,9},{9,8},{10,11... | collective-permute-start | bytes 786440 | tf_op jit(solution)/shard_map/ppermute | solution.py:19
  30.1 10.2 %collective-permute-start.7 = (bf16[8,128,128]{2,1,0:T(8,128)(2,1)S(1)}, bf16[8,128,128]{2,1,0:T(8,128)(2,1)S(1)}, u32[]{:S(2)}, u32[]{:S(2)}) collective-permute-start(bf16[8,128,128]{2,1,0:T(8,128)(2,1)S(1)} %add_convert_fusion.3), channel_id=1, source_target_pairs={{0,2},{1,3},{6,4},{7,5},{8,10},{9,11},{14,12},{15,13},{16,18},{17,... | collective-permute-start | bytes 786440 | tf_op jit(solution)/shard_map/ppermute | solution.py:28
  33.3 12.2 %collective-permute-start.3 = (bf16[8,128,128]{2,1,0:T(8,128)(2,1)}, bf16[8,128,128]{2,1,0:T(8,128)(2,1)S(1)}, u32[]{:S(2)}, u32[]{:S(2)}) collective-permute-start(bf16[8,128,128]{2,1,0:T(8,128)(2,1)} %get-tuple-element.30), channel_id=1, source_target_pairs={{0,1},{1,0},{2,3},{3,2},{4,5},{5,4},{6,7},{7,6},{8,9},{9,8},{10,11... | collective-permute-start | bytes 786440 | tf_op jit(solution)/shard_map/ppermute | solution.py:19
  35.4 10.1 %collective-permute-start.5 = (bf16[8,128,128]{2,1,0:T(8,128)(2,1)S(1)}, bf16[8,128,128]{2,1,0:T(8,128)(2,1)S(1)}, u32[]{:S(2)}, u32[]{:S(2)}) collective-permute-start(bf16[8,128,128]{2,1,0:T(8,128)(2,1)S(1)} %add_convert_fusion.3), channel_id=1, source_target_pairs={{2,4},{3,5},{4,2},{5,3},{10,12},{11,13},{12,10},{13,11},{18,20},{1... | collective-permute-start | bytes 786440 | tf_op jit(solution)/shard_map/ppermute | solution.py:28
  37.1 8.7 %collective-permute-start.10 = (bf16[8,128,128]{2,1,0:T(8,128)(2,1)S(1)}, bf16[8,128,128]{2,1,0:T(8,128)(2,1)S(1)}, u32[]{:S(2)}, u32[]{:S(2)}) collective-permute-start(bf16[8,128,128]{2,1,0:T(8,128)(2,1)S(1)} %add_convert_fusion.1), channel_id=1, source_target_pairs={{0,2},{1,3},{2,0},{3,1},{4,6},{5,7},{6,4},{7,5},{8,10},{9,11},{10,... | collective-permute-start | bytes 786440 | tf_op jit(solution)/shard_map/ppermute | solution.py:19
  41.3 14.0 %collective-permute-start.8 = (bf16[8,128,128]{2,1,0:T(8,128)(2,1)S(1)}, bf16[8,128,128]{2,1,0:T(8,128)(2,1)S(1)}, u32[]{:S(2)}, u32[]{:S(2)}) collective-permute-start(bf16[8,128,128]{2,1,0:T(8,128)(2,1)S(1)} %add_convert_fusion.2), channel_id=1, source_target_pairs={{0,4},{1,5},{2,6},{3,7},{4,0},{5,1},{6,2},{7,3},{8,12},{9,13},{10,... | collective-permute-start | bytes 786440 | tf_op jit(solution)/shard_map/ppermute | solution.py:19
  59.3 15.2 %collective-permute-start.14 = (bf16[8,128,128]{2,1,0:T(8,128)(2,1)}, bf16[8,128,128]{2,1,0:T(8,128)(2,1)S(1)}, u32[]{:S(2)}, u32[]{:S(2)}) collective-permute-start(bf16[8,128,128]{2,1,0:T(8,128)(2,1)} %get-tuple-element.41.refs_5_), channel_id=1, source_target_pairs={{0,4},{1,5},{2,6},{3,7},{4,0},{5,1},{6,2},{7,3},{8,12},{9,13},{10,... | collective-permute-start | bytes 786440 | tf_op jit(solution)/shard_map/ppermute | solution.py:19
  59.3 1.5 %collective-permute-start.20 = (f32[128,128]{1,0:T(8,128)}, f32[128,128]{1,0:T(8,128)S(1)}, u32[]{:S(2)}, u32[]{:S(2)}) collective-permute-start(f32[128,128]{1,0:T(8,128)} %get-tuple-element.39), channel_id=1, source_target_pairs={{0,8},{8,0},{16,24},{24,16},{1,9},{9,1},{17,25},{25,17},{2,10},{10... | collective-permute-start | bytes 196616 | tf_op jit(solution)/shard_map/ppermute | solution.py:19
  61.6 14.2 %collective-permute-start.21 = (f32[128,128]{1,0:T(8,128)S(1)}, f32[128,128]{1,0:T(8,128)S(1)}, u32[]{:S(2)}, u32[]{:S(2)}) collective-permute-start(f32[128,128]{1,0:T(8,128)S(1)} %add.41), channel_id=1, source_target_pairs={{0,16},{8,24},{16,0},{24,8},{1,17},{9,25},{17,1},{25,9},{2,18},{10... | collective-permute-start | bytes 196616 | tf_op jit(solution)/shard_map/ppermute | solution.py:19
  63.4 23.5 %collective-permute-start.16 = (bf16[8,128,128]{2,1,0:T(8,128)(2,1)}, bf16[8,128,128]{2,1,0:T(8,128)(2,1)S(1)}, u32[]{:S(2)}, u32[]{:S(2)}) collective-permute-start(bf16[8,128,128]{2,1,0:T(8,128)(2,1)} %get-tuple-element.41.refs_5_), channel_id=1, source_target_pairs={{2,4},{3,5},{4,2},{5,3},{10,12},{11,13},{12,10},{13,11},{18,20},{1... | collective-permute-start | bytes 786440 | tf_op jit(solution)/shard_map/ppermute | solution.py:28
  64.1 23.6 %collective-permute-start.12 = (bf16[8,128,128]{2,1,0:T(8,128)(2,1)}, bf16[8,128,128]{2,1,0:T(8,128)(2,1)S(1)}, u32[]{:S(2)}, u32[]{:S(2)}) collective-permute-start(bf16[8,128,128]{2,1,0:T(8,128)(2,1)} %get-tuple-element.41.refs_5_), channel_id=1, source_target_pairs={{0,2},{1,3},{2,0},{3,1},{4,6},{5,7},{6,4},{7,5},{8,10},{9,11},{10,... | collective-permute-start | bytes 786440 | tf_op jit(solution)/shard_map/ppermute | solution.py:19
  74.5 35.4 %copy-start.6 = (bf16[8,128,128]{2,1,0:T(8,128)(2,1)}, bf16[8,128,128]{2,1,0:T(8,128)(2,1)S(1)}, u32[]{:S(2)}) copy-start(bf16[8,128,128]{2,1,0:T(8,128)(2,1)S(1)} %collective-permute-done.14.refs_9_) | copy-start | bytes 786436
  74.5 17.5 %collective-permute-start.17 = (bf16[8,128,128]{2,1,0:T(8,128)(2,1)S(1)}, bf16[8,128,128]{2,1,0:T(8,128)(2,1)S(1)}, u32[]{:S(2)}, u32[]{:S(2)}) collective-permute-start(bf16[8,128,128]{2,1,0:T(8,128)(2,1)S(1)} %collective-permute-done.14.refs_9_), channel_id=1, source_target_pairs={{2,0},{3,1},{4,6},{5,7},{10,8},{11,9},{12,14},{13,15},{18,16},{19,... | collective-permute-start | bytes 786440 | tf_op jit(solution)/shard_map/ppermute | solution.py:28
  75.8 4.3 %collective-permute-start.22 = (f32[128,128]{1,0:T(8,128)S(1)}, f32[128,128]{1,0:T(8,128)S(1)}, u32[]{:S(2)}, u32[]{:S(2)}) collective-permute-start(f32[128,128]{1,0:T(8,128)S(1)} %add.42), channel_id=1, source_target_pairs={{0,1},{1,0},{2,3},{3,2},{4,5},{5,4},{6,7},{7,6},{8,9},{9,8},{10,11... | collective-permute-start | bytes 196616 | tf_op jit(solution)/shard_map/ppermute | solution.py:19
  80.2 5.3 %collective-permute-start.23 = (f32[128,128]{1,0:T(8,128)S(1)}, f32[128,128]{1,0:T(8,128)S(1)}, u32[]{:S(2)}, u32[]{:S(2)}) collective-permute-start(f32[128,128]{1,0:T(8,128)S(1)} %add.43), channel_id=1, source_target_pairs={{0,2},{1,3},{2,0},{3,1},{4,6},{5,7},{6,4},{7,5},{8,10},{9,11},{10,... | collective-permute-start | bytes 196616 | tf_op jit(solution)/shard_map/ppermute | solution.py:19
  85.5 5.2 %collective-permute-start.24 = (f32[128,128]{1,0:T(8,128)S(1)}, f32[128,128]{1,0:T(8,128)S(1)}, u32[]{:S(2)}, u32[]{:S(2)}) collective-permute-start(f32[128,128]{1,0:T(8,128)S(1)} %add.44), channel_id=1, source_target_pairs={{0,4},{1,5},{2,6},{3,7},{4,0},{5,1},{6,2},{7,3},{8,12},{9,13},{10,... | collective-permute-start | bytes 196616 | tf_op jit(solution)/shard_map/ppermute | solution.py:19
  85.6 10.4 %collective-permute-start.11 = (bf16[8,128,128]{2,1,0:T(8,128)(2,1)}, bf16[8,128,128]{2,1,0:T(8,128)(2,1)S(1)}, u32[]{:S(2)}, u32[]{:S(2)}) collective-permute-start(bf16[8,128,128]{2,1,0:T(8,128)(2,1)} %get-tuple-element.41.refs_5_), channel_id=1, source_target_pairs={{0,1},{1,0},{2,3},{3,2},{4,5},{5,4},{6,7},{7,6},{8,9},{9,8},{10,11... | collective-permute-start | bytes 786440 | tf_op jit(solution)/shard_map/ppermute | solution.py:19
  86.9 22.9 %copy-start.8 = (bf16[8,128,128]{2,1,0:T(8,128)(2,1)}, bf16[8,128,128]{2,1,0:T(8,128)(2,1)S(1)}, u32[]{:S(2)}) copy-start(bf16[8,128,128]{2,1,0:T(8,128)(2,1)S(1)} %collective-permute-done.16.refs_11_) | copy-start | bytes 786436
  86.9 13.7 %collective-permute-start.15 = (bf16[8,128,128]{2,1,0:T(8,128)(2,1)S(1)}, bf16[8,128,128]{2,1,0:T(8,128)(2,1)S(1)}, u32[]{:S(2)}, u32[]{:S(2)}) collective-permute-start(bf16[8,128,128]{2,1,0:T(8,128)(2,1)S(1)} %collective-permute-done.14.refs_9_), channel_id=1, source_target_pairs={{0,1},{1,0},{2,3},{3,2},{4,5},{5,4},{6,7},{7,6},{8,9},{9,8},{10,11... | collective-permute-start | bytes 786440 | tf_op jit(solution)/shard_map/ppermute | solution.py:19
  87.7 22.2 %copy-start.10 = (bf16[8,128,128]{2,1,0:T(8,128)(2,1)}, bf16[8,128,128]{2,1,0:T(8,128)(2,1)S(1)}, u32[]{:S(2)}) copy-start(bf16[8,128,128]{2,1,0:T(8,128)(2,1)S(1)} %collective-permute-done.12.refs_7_) | copy-start | bytes 786436
  87.7 8.3 %collective-permute-start.18 = (bf16[8,128,128]{2,1,0:T(8,128)(2,1)S(1)}, bf16[8,128,128]{2,1,0:T(8,128)(2,1)S(1)}, u32[]{:S(2)}, u32[]{:S(2)}) collective-permute-start(bf16[8,128,128]{2,1,0:T(8,128)(2,1)S(1)} %collective-permute-done.16.refs_11_), channel_id=1, source_target_pairs={{2,3},{3,2},{4,5},{5,4},{10,11},{11,10},{12,13},{13,12},{18,19},{1... | collective-permute-start | bytes 786440 | tf_op jit(solution)/shard_map/ppermute | solution.py:28
  90.7 15.5 %collective-permute-start.13 = (bf16[8,128,128]{2,1,0:T(8,128)(2,1)S(1)}, bf16[8,128,128]{2,1,0:T(8,128)(2,1)S(1)}, u32[]{:S(2)}, u32[]{:S(2)}) collective-permute-start(bf16[8,128,128]{2,1,0:T(8,128)(2,1)S(1)} %collective-permute-done.12.refs_7_), channel_id=1, source_target_pairs={{0,1},{1,0},{2,3},{3,2},{4,5},{5,4},{6,7},{7,6},{8,9},{9,8},{10,11... | collective-permute-start | bytes 786440 | tf_op jit(solution)/shard_map/ppermute | solution.py:19
  92.0 17.8 %copy-start.12 = (bf16[8,128,128]{2,1,0:T(8,128)(2,1)}, bf16[8,128,128]{2,1,0:T(8,128)(2,1)S(1)}, u32[]{:S(2)}) copy-start(bf16[8,128,128]{2,1,0:T(8,128)(2,1)S(1)} %collective-permute-done.17.refs_12_) | copy-start | bytes 786436
  92.0 17.8 %collective-permute-start.19 = (bf16[8,128,128]{2,1,0:T(8,128)(2,1)S(1)}, bf16[8,128,128]{2,1,0:T(8,128)(2,1)S(1)}, u32[]{:S(2)}, u32[]{:S(2)}) collective-permute-start(bf16[8,128,128]{2,1,0:T(8,128)(2,1)S(1)} %collective-permute-done.17.refs_12_), channel_id=1, source_target_pairs={{0,1},{1,0},{6,7},{7,6},{8,9},{9,8},{14,15},{15,14},{16,17},{17,16... | collective-permute-start | bytes 786440 | tf_op jit(solution)/shard_map/ppermute | solution.py:28
  117.1 1.8 %collective-permute-start.25 = (bf16[8,128,128]{2,1,0:T(8,128)(2,1)}, bf16[8,128,128]{2,1,0:T(8,128)(2,1)S(1)}, u32[]{:S(2)}, u32[]{:S(2)}) collective-permute-start(bf16[8,128,128]{2,1,0:T(8,128)(2,1)} %get-tuple-element.53), channel_id=1, source_target_pairs={{0,8},{8,0},{16,24},{24,16},{1,9},{9,1},{17,25},{25,17},{2,10},{10... | collective-permute-start | bytes 786440 | tf_op jit(solution)/shard_map/ppermute | solution.py:19
  117.2 5.2 %collective-permute-start.27 = (bf16[8,128,128]{2,1,0:T(8,128)(2,1)}, bf16[8,128,128]{2,1,0:T(8,128)(2,1)S(1)}, u32[]{:S(2)}, u32[]{:S(2)}) collective-permute-start(bf16[8,128,128]{2,1,0:T(8,128)(2,1)} %get-tuple-element.54), channel_id=1, source_target_pairs={{0,8},{8,0},{16,24},{24,16},{1,9},{9,1},{17,25},{25,17},{2,10},{10... | collective-permute-start | bytes 786440 | tf_op jit(solution)/shard_map/ppermute | solution.py:19
  120.0 9.0 %collective-permute-start.26 = (bf16[8,128,128]{2,1,0:T(8,128)(2,1)S(1)}, bf16[8,128,128]{2,1,0:T(8,128)(2,1)S(1)}, u32[]{:S(2)}, u32[]{:S(2)}) collective-permute-start(bf16[8,128,128]{2,1,0:T(8,128)(2,1)S(1)} %add_convert_fusion), channel_id=1, source_target_pairs={{0,16},{8,24},{16,0},{24,8},{1,17},{9,25},{17,1},{25,9},{2,18},{10... | collective-permute-start | bytes 786440 | tf_op jit(solution)/shard_map/ppermute | solution.py:19
  (14 other events, 81.9 us)
